TPU v7x, 32 devices: a whole 2x2x4 slice. The times are simulated.
32 devices in a mesh: zero: 8 (over z, y), width: 4 (over x, core).
Axes of the slice: x: 2, y: 2, z: 4, core: 2. Of those that a mesh axis runs over, the one named last changes fastest.
Arguments:
- train_query: float32 [7168, 7168], P('zero', 'width'), may hold values from -0.09375 to 0.09375
- slow_query: float32 [7168, 7168], P('zero', 'width'), may hold values from -0.0625 to 0.0625
- train_key: float32 [7168, 1024], P('zero', 'width'), may hold values from -0.09375 to 0.09375
- slow_key: float32 [7168, 1024], P('zero', 'width'), may hold values from -0.0625 to 0.0625
- train_value: float32 [7168, 1024], P('zero', 'width'), may hold values from -0.09375 to 0.09375
- slow_value: float32 [7168, 1024], P('zero', 'width'), may hold values from -0.0625 to 0.0625
- norm_train: float32 [7168], P(('zero', 'width')), may hold values from 0.25 to 1.75
- norm_step: float32 [7168], P(('zero', 'width')), may hold values from -0.3 to 0.3
Outputs:
- ready_query: bfloat16 [7168, 7168], P(None, 'width')
- ready_key: bfloat16 [7168, 1024], P(None, 'width')
- ready_value: bfloat16 [7168, 1024], P(None, 'width')
- scale_query: float32 [7168], P('width')
- scale_key: float32 [1024], P('width')
- scale_value: float32 [1024], P('width')
- serve_norm: bfloat16 [7168], replicated
- latest_query: float32 [7168, 7168], P('zero', 'width')
- latest_key: float32 [7168, 1024], P('zero', 'width')
- latest_value: float32 [7168, 1024], P('zero', 'width')
All inputs are finite; a program needn't handle non-finite values.
Results may differ from a plain program's by a relative error of at most 0.0004.
Values may be sent and summed in bfloat16 or wider, within the bound.
A program may use at most 128 MiB of HBM per device.

v0:
```python
import functools

import jax
import jax.numpy as jnp
from jax import lax
from jax.experimental import pallas as pl
from jax.experimental.pallas import tpu as pltpu
from jax.sharding import PartitionSpec as P

keep_rate = 0.5
MESH = pl.DeviceIdType.MESH


def grid_of(count):
    fast = 1
    while (2 * fast) ** 2 <= count and count % (2 * fast) == 0:
        fast *= 2
    return count // fast, fast


def node_at(place, slow, fast):
    if fast == 1:
        return place
    deep = slow - 1
    back = place // (deep * fast)
    column = place // deep
    step = place % deep
    step = step + (column % 2) * (deep - 1 - 2 * step)
    z = (1 - back) * (1 + step)
    y = (1 - back) * column + back * (fast - 1 - (place - deep * fast))
    return z * fast + y


def place_of(node, slow, fast):
    if fast == 1:
        return node
    deep = slow - 1
    z, y = node // fast, node % fast
    out = (z + slow - 1) // slow
    step = z - 1
    step = step + (y % 2) * (deep - 1 - 2 * step)
    return out * (y * deep + step) + (1 - out) * (deep * fast + fast - 1 - y)


def gather_kernel(
    count, across, width, half, tile,
    tq, sq, tk, sk, tv, sv, norm_train, norm_step,
    rq, rk, rv, lq, lk, lv, scale_q, scale_k, scale_v, norm_all,
    itq, isq, itk, isk, itv, isv, stats_a, stats_b,
    load_sem, stat_send, stat_recv, near_send, near_recv, far_send, far_recv,
    send_sem, recv_sem,
):
    me, side = lax.axis_index("zero"), lax.axis_index("width")
    slow, fast = grid_of(count)
    place = place_of(me, slow, fast)
    ahead = node_at(lax.rem(place + 1, count), slow, fast)
    behind = node_at(lax.rem(place + count - 1, count), slow, fast)
    rows = 2 * half
    trains, slows = ((tq, itq), (tk, itk), (tv, itv)), ((sq, isq), (sk, isk), (sv, isv))
    latest, ready, scales = (lq, lk, lv), (rq, rk, rv), (scale_q, scale_k, scale_v)
    groups = [(1, 0), (2, 0)] + [(0, c) for c in range(tq.shape[1] // width)]

    def columns(c):
        return pl.ds(c * width, width)

    loads = []
    for i, (which, c) in enumerate(groups):
        pair = []
        for j, arrays in enumerate((trains, slows)):
            far, near = arrays[which]
            pair.append(
                pltpu.make_async_copy(far.at[:, columns(c)], near.at[:, columns(c)], load_sem.at[j, i])
            )
            pair[-1].start()
        loads.append(pair)

    barrier = pltpu.get_barrier_semaphore()
    for k in range(1, count):
        pl.semaphore_signal(
            barrier, inc=1, device_id=(lax.rem(me + k, count), side), device_id_type=MESH
        )
    for k in range(1, across):
        pl.semaphore_signal(
            barrier, inc=1, device_id=(me, lax.rem(side + k, across)), device_id_type=MESH
        )
    mine = me * across + side
    norm_all[mine] = norm_train[...] + norm_step[...]

    def stat_copy(part, k):
        stats = (stats_a, stats_b)[part]
        return pltpu.make_async_remote_copy(
            src_ref=stats.at[me], dst_ref=stats.at[me],
            send_sem=stat_send.at[part, k - 1], recv_sem=stat_recv.at[part, k - 1],
            device_id=(lax.rem(me + k, count), side), device_id_type=MESH,
        )

    def near_copy(k):
        return pltpu.make_async_remote_copy(
            src_ref=norm_all.at[mine], dst_ref=norm_all.at[mine],
            send_sem=near_send.at[k - 1], recv_sem=near_recv.at[k - 1],
            device_id=(me, lax.rem(side + k, across)), device_id_type=MESH,
        )

    def far_copy(k):
        at = pl.ds(me * across, across)
        return pltpu.make_async_remote_copy(
            src_ref=norm_all.at[at], dst_ref=norm_all.at[at],
            send_sem=far_send.at[k - 1], recv_sem=far_recv.at[k - 1],
            device_id=(lax.rem(me + k, count), side), device_id_type=MESH,
        )

    def average(i, stats, c_out):
        which, c = groups[i]
        for load in loads[i]:
            load.wait()

        def step(t, total):
            at = pl.ds(pl.multiple_of(t * tile, 16), tile)
            value = (
                keep_rate * slows[which][1][at, columns(c)]
                + (1.0 - keep_rate) * trains[which][1][at, columns(c)]
            )
            latest[which][at, columns(c)] = value
            return total + jnp.sum((value * value).reshape(tile // 8, 8, width), axis=0)

        total = lax.fori_loop(0, rows // tile, step, jnp.zeros((8, width), jnp.float32))
        stats[me, :, columns(c_out)] = jnp.sum(total, axis=0, keepdims=True)

    def ring_copy(owner, step, i, way):
        which, c = groups[i]
        spot = pl.ds(pl.multiple_of(owner * rows + way * half, 16), half)
        piece = ready[which].at[spot, columns(c)]
        return pltpu.make_async_remote_copy(
            src_ref=piece, dst_ref=piece,
            send_sem=send_sem.at[way, step, i], recv_sem=recv_sem.at[way, step, i],
            device_id=(behind if way else ahead, side), device_id_type=MESH,
        )

    def owner_of(step, way):
        return node_at(lax.rem(place + (step if way else count - step), count), slow, fast)

    def send_own(i):
        which, c = groups[i]
        scale = scales[which][:, columns(c)]
        for way in range(2):

            def step(t, carry):
                at = pl.multiple_of(way * half + t * tile, 16)
                home = pl.multiple_of(me * rows + at, 16)
                ready[which][pl.ds(home, tile), columns(c)] = (
                    latest[which][pl.ds(at, tile), columns(c)] / scale
                ).astype(jnp.bfloat16)
                return carry

            lax.fori_loop(0, half // tile, step, 0)
            ring_copy(me, 0, i, way).start()

    def finish(part, members):
        stats = (stats_a, stats_b)[part]
        for k in range(1, count):
            stat_copy(part, k).wait_recv()
        total = stats[0]
        for k in range(1, count):
            total = total + stats[k]
        total = jnp.sqrt(total)
        at = 0
        for which in members:
            wide = scales[which].shape[1]
            scales[which][...] = total[:, at : at + wide]
            at += wide

    average(0, stats_a, 0)
    average(1, stats_a, 1)
    pl.semaphore_wait(barrier, count + across - 2)
    for k in range(1, count):
        stat_copy(0, k).start()
    for k in range(1, across):
        near_copy(k).start()
    early = 2 + (len(groups) - 2) // 2 + 1
    for i in range(2, early):
        average(i, stats_b, groups[i][1])
    finish(0, (1, 2))
    send_own(0)
    send_own(1)
    for i in range(early, len(groups)):
        average(i, stats_b, groups[i][1])
    for k in range(1, count):
        stat_copy(1, k).start()
    finish(1, (0,))
    for i in range(2, len(groups)):
        send_own(i)
    for k in range(1, across):
        near_copy(k).wait_recv()
    for k in range(1, count):
        far_copy(k).start()

    def forward(step, carry):
        owners = owner_of(step, 0), owner_of(step, 1)
        for i in range(len(groups)):
            for way in range(2):
                ring_copy(owners[way], step - 1, i, way).wait_recv()
                ring_copy(owners[way], step, i, way).start()
        return carry

    lax.fori_loop(1, count - 1, forward, 0)
    for i in range(len(groups)):
        for way in range(2):
            ring_copy(owner_of(count - 1, way), count - 2, i, way).wait_recv()

    def drain(step, carry):
        for i in range(len(groups)):
            for way in range(2):
                ring_copy(owner_of(step, way), step, i, way).wait_send()
        return carry

    lax.fori_loop(0, count - 1, drain, 0)
    for k in range(1, count):
        stat_copy(0, k).wait_send()
        stat_copy(1, k).wait_send()
        far_copy(k).wait()
    for k in range(1, across):
        near_copy(k).wait_send()


def gather(arrays, norm_train, norm_step, count, across):
    rows = arrays[0].shape[0]
    wides = [a.shape[1] for a in arrays[::2]]
    half = rows // 2
    width = wides[1]
    tile = 112 if half % 112 == 0 else 16
    n = sum(wides) // width
    piece = norm_train.shape[0]
    hbm = pl.BlockSpec(memory_space=pl.ANY)
    vmem = pl.BlockSpec(memory_space=pltpu.VMEM)
    dma = pltpu.SemaphoreType.DMA
    return pl.pallas_call(
        functools.partial(gather_kernel, count, across, width, half, tile),
        in_specs=[hbm] * 6 + [vmem] * 2,
        out_specs=[vmem] * 10,
        out_shape=[pltpu.VMEM((count * rows, w), jnp.bfloat16) for w in wides]
        + [pltpu.VMEM((rows, w), jnp.float32) for w in wides]
        + [pltpu.VMEM((1, w), jnp.float32) for w in wides]
        + [jax.ShapeDtypeStruct((count * across, 1, piece), jnp.float32)],
        scratch_shapes=[pltpu.VMEM(a.shape, jnp.float32) for a in arrays]
        + [
            pltpu.VMEM((count, 1, 2 * width), jnp.float32),
            pltpu.VMEM((count, 1, wides[0]), jnp.float32),
            dma((2, n)),
            dma((2, count - 1)),
            dma((2, count - 1)),
            dma((across - 1,)),
            dma((across - 1,)),
            dma((count - 1,)),
            dma((count - 1,)),
            dma((2, count - 1, n)),
            dma((2, count - 1, n)),
        ],
        compiler_params=pltpu.CompilerParams(
            collective_id=0, has_side_effects=True,
            vmem_limit_bytes=4 * sum(a.size for a in arrays) + 2**21,
        ),
    )(*arrays, norm_train.reshape(1, piece), norm_step.reshape(1, piece))


def store_kernel(cuts, count, *refs):
    wide, thin = count, (len(refs) - 1) // 2 - count
    wide_in, scale_in = refs[:wide], refs[wide : wide + thin]
    wide_out, scale_out = refs[wide + thin : 2 * wide + thin], refs[2 * wide + thin : -1]
    sem = refs[-1]
    copies = []
    for i, (source, target) in enumerate(zip(wide_in, wide_out)):
        size = source.shape[0] // cuts
        for c in range(cuts):
            at = pl.ds(c * size, size)
            copies.append(pltpu.make_async_copy(source.at[at], target.at[at], sem.at[i, c]))
            copies[-1].start()
    for source, target in zip(scale_in, scale_out):
        target[...] = source[0, :]
    for copy in copies:
        copy.wait()


def store(arrays, scales):
    cuts = 8
    hbm = pl.BlockSpec(memory_space=pl.ANY)
    vmem = pl.BlockSpec(memory_space=pltpu.VMEM)
    return pl.pallas_call(
        functools.partial(store_kernel, cuts, len(arrays)),
        in_specs=[vmem] * (len(arrays) + len(scales)),
        out_specs=[hbm] * len(arrays) + [vmem] * len(scales),
        out_shape=[jax.ShapeDtypeStruct(a.shape, a.dtype) for a in arrays]
        + [jax.ShapeDtypeStruct((s.shape[1],), s.dtype) for s in scales],
        scratch_shapes=[pltpu.SemaphoreType.DMA((len(arrays), cuts))],
        compiler_params=pltpu.CompilerParams(vmem_limit_bytes=2**20),
    )(*arrays, *scales)


def solution(mesh):
    count, across = mesh.shape["zero"], mesh.shape["width"]

    def body(
        train_query, slow_query, train_key, slow_key, train_value, slow_value, norm_train, norm_step
    ):
        *arrays, norm = gather(
            (train_query, slow_query, train_key, slow_key, train_value, slow_value),
            norm_train, norm_step, count, across,
        )
        outs = store(arrays[:1], ()) + store(arrays[1:6], arrays[6:])
        serve_norm = norm.astype(jnp.bfloat16).reshape(-1)
        return (*outs[:3], *outs[6:], serve_norm, *outs[3:6])

    in_specs = (P("zero", "width"),) * 6 + (P(("zero", "width")),) * 2
    out_specs = (
        (P(None, "width"),) * 3 + (P("width"),) * 3 + (P(),) + (P("zero", "width"),) * 3
    )
    return jax.shard_map(body, mesh=mesh, in_specs=in_specs, out_specs=out_specs, check_vma=False)
```

profile of v0, /device:TPU:0, one launch (start us, length us, event | category | flops | bytes accessed | tf_op | source)
XLA Modules:
  0.0 354.0 jit_solution(16134115585865596253)
XLA Ops:
  0.6 326.5 %shard_map.159 = (bf16[7168,1792]{1,0:T(8,128)(2,1)S(1)}, bf16[7168,256]{1,0:T(8,128)(2,1)S(1)}, bf16[7168,256]{1,0:T(8,128)(2,1)S(1)}, f32[896,1792]{1,0:T(8,12...) custom-call(f32[896,1792]{1,0:T(8,128)} %tq.1, ...), custom_call_target="tpu_custom_call" | custom-call | tf_op jit(solution)/shard_map/pallas_call | solution.py:236
  327.1 0.0 copy-start
  327.1 0.0 copy-start.2
  327.2 0.0 copy-start.4
  327.2 0.0 copy-start.6
  327.2 8.5 %shard_map.160 = bf16[7168,1792]{1,0:T(8,128)(2,1)} custom-call(bf16[7168,1792]{1,0:T(8,128)(2,1)S(1)} %get-tuple-element.28.refs_0_), custom_call_target="tpu_custom_call" | custom-call | tf_op jit(solution)/shard_map/pallas_call | solution.py:287
  335.7 1.9 copy-done
  337.6 1.2 copy-done.2
  338.8 1.1 copy-done.4
  339.9 0.0 copy-done.6
  339.9 0.1 convert_reduce_fusion
  340.0 0.7 reshape.31
  340.7 0.0 copy-start.1
  340.7 2.8 copy-done.1
  343.5 0.0 copy-start.3
  343.5 2.0 copy-done.3
  345.6 0.0 copy-start.5
  345.6 2.0 copy-done.5
  347.6 6.4 %shard_map.161 = (bf16[7168,256]{1,0:T(8,128)(2,1)}, bf16[7168,256]{1,0:T(8,128)(2,1)}, f32[896,1792]{1,0:T(8,128)}, f32[896,256]{1,0:T(8,128)}, f32[896,256]{1,...) custom-call(bf16[7168,256]{1,0:T(8,128)(2,1)S(1)} %copy-done.3, bf16[7168,256]{1,0:T(8,128)(2,1)S(1)} %copy-done.5, ...), custom_call_target="tpu_custom_call" | custom-call | tf_op jit(solution)/shard_map/pallas_call | solution.py:287
Async XLA Ops:
  327.1 10.5 %copy-start = (f32[896,1792]{1,0:T(8,128)}, f32[896,1792]{1,0:T(8,128)S(1)}, u32[]{:S(2)}) copy-start(f32[896,1792]{1,0:T(8,128)S(1)} %get-tuple-element.31.refs_2_) | copy-start | bytes 19267588
  327.1 11.7 %copy-start.2 = (bf16[7168,256]{1,0:T(8,128)(2,1)}, bf16[7168,256]{1,0:T(8,128)(2,1)S(1)}, u32[]{:S(2)}) copy-start(bf16[7168,256]{1,0:T(8,128)(2,1)S(1)} %get-tuple-element.29.refs_0_) | copy-start | bytes 11010052
  327.2 12.8 %copy-start.4 = (bf16[7168,256]{1,0:T(8,128)(2,1)}, bf16[7168,256]{1,0:T(8,128)(2,1)S(1)}, u32[]{:S(2)}) copy-start(bf16[7168,256]{1,0:T(8,128)(2,1)S(1)} %get-tuple-element.30.refs_1_) | copy-start | bytes 11010052
  327.2 12.7 %copy-start.6 = (f32[32,1,224]{2,1,0:T(1,128)S(1)}, f32[32,1,224]{2,1,0:T(1,128)}, u32[]{:S(2)}) copy-start(f32[32,1,224]{2,1,0:T(1,128)} %get-tuple-element.42) | copy-start | bytes 86020
  340.7 2.8 copy-start.1
  343.5 2.0 copy-start.3
  345.6 2.0 copy-start.5
where the time goes:
time: 354 us
  Pallas kernels  341 us (96%)
  local copies, waits for them, and re-layouts  11.8 us (3%)
    pallas_call x1, Pallas kernels, gather(): pl.pallas_call(functools.partial(gather_kernel, count, across, width, hal...  326 us
    pallas_call x2, Pallas kernels, store(): pl.pallas_call(functools.partial(store_kernel, cuts, len(arrays)), in_spe...  14.9 us
    unnamed x14, local copies, waits for them, and re-layouts  11.1 us

commit v1 on v0

v1 whole, which is shorter than its diff:
```python
import functools

import jax
import jax.numpy as jnp
from jax import lax
from jax.experimental import pallas as pl
from jax.experimental.pallas import tpu as pltpu
from jax.sharding import PartitionSpec as P

keep_rate = 0.5
MESH = pl.DeviceIdType.MESH


def grid_of(count):
    fast = 1
    while (2 * fast) ** 2 <= count and count % (2 * fast) == 0:
        fast *= 2
    return count // fast, fast


def node_at(place, slow, fast):
    if fast == 1:
        return place
    deep = slow - 1
    back = place // (deep * fast)
    column = place // deep
    step = place % deep
    step = step + (column % 2) * (deep - 1 - 2 * step)
    z = (1 - back) * (1 + step)
    y = (1 - back) * column + back * (fast - 1 - (place - deep * fast))
    return z * fast + y


def place_of(node, slow, fast):
    if fast == 1:
        return node
    deep = slow - 1
    z, y = node // fast, node % fast
    out = (z + slow - 1) // slow
    step = z - 1
    step = step + (y % 2) * (deep - 1 - 2 * step)
    return out * (y * deep + step) + (1 - out) * (deep * fast + fast - 1 - y)


def ring_of(count):
    me = lax.axis_index("zero")
    slow, fast = grid_of(count)
    place = place_of(me, slow, fast)

    def node(step):
        return node_at(lax.rem(place + count + step, count), slow, fast)

    return me, node


def gather_kernel(
    count, across, width, half, tile, groups, parts,
    tq, sq, tk, sk, tv, sv, norm_train, norm_step,
    rq, rk, rv, lq, lk, lv, scale_q, scale_k, scale_v, norm_all,
    itq, isq, itk, isk, itv, isv, stats,
    load_sem, stat_send, stat_recv, near_send, near_recv, far_send, far_recv,
    send_sem, recv_sem,
):
    me, node = ring_of(count)
    side = lax.axis_index("width")
    late = lax.rem(side, 2) == 0
    ahead, behind = node(1), node(-1)
    rows = 2 * half
    trains, slows = ((tq, itq), (tk, itk), (tv, itv)), ((sq, isq), (sk, isk), (sv, isv))
    latest, ready, scales = (lq, lk, lv), (rq, rk, rv), (scale_q, scale_k, scale_v)

    def columns(c):
        return pl.ds(c * width, width)

    def early(i, action):
        if groups[i][0] == 2:
            pl.when(jnp.logical_not(late))(action)
        else:
            action()

    barrier = pltpu.get_barrier_semaphore()
    for k in range(1, count):
        pl.semaphore_signal(
            barrier, inc=1, device_id=(lax.rem(me + k, count), side), device_id_type=MESH
        )
    for k in range(1, across):
        pl.semaphore_signal(
            barrier, inc=1, device_id=(me, lax.rem(side + k, across)), device_id_type=MESH
        )

    loads = []
    for i, (which, c) in enumerate(groups):
        pair = []
        for j, arrays in enumerate((trains, slows)):
            far, near = arrays[which]
            pair.append(
                pltpu.make_async_copy(far.at[:, columns(c)], near.at[:, columns(c)], load_sem.at[j, i])
            )
            pair[-1].start()
        loads.append(pair)
    mine = me * across + side
    norm_all[mine] = norm_train[...] + norm_step[...]

    def stat_copy(part, k):
        first, last = parts[part]
        piece = stats.at[me, :, pl.ds(first * width, (last - first) * width)]
        return pltpu.make_async_remote_copy(
            src_ref=piece, dst_ref=piece,
            send_sem=stat_send.at[part, k - 1], recv_sem=stat_recv.at[part, k - 1],
            device_id=(lax.rem(me + k, count), side), device_id_type=MESH,
        )

    def near_copy(k):
        return pltpu.make_async_remote_copy(
            src_ref=norm_all.at[mine], dst_ref=norm_all.at[mine],
            send_sem=near_send.at[k - 1], recv_sem=near_recv.at[k - 1],
            device_id=(me, lax.rem(side + k, across)), device_id_type=MESH,
        )

    def far_copy(k):
        at = pl.ds(me * across, across)
        return pltpu.make_async_remote_copy(
            src_ref=norm_all.at[at], dst_ref=norm_all.at[at],
            send_sem=far_send.at[k - 1], recv_sem=far_recv.at[k - 1],
            device_id=(lax.rem(me + k, count), side), device_id_type=MESH,
        )

    def average(i):
        which, c = groups[i]
        for load in loads[i]:
            load.wait()

        def step(t, total):
            at = pl.ds(pl.multiple_of(t * tile, 16), tile)
            value = (
                keep_rate * slows[which][1][at, columns(c)]
                + (1.0 - keep_rate) * trains[which][1][at, columns(c)]
            )
            latest[which][at, columns(c)] = value
            return total + jnp.sum((value * value).reshape(tile // 8, 8, width), axis=0)

        total = lax.fori_loop(0, rows // tile, step, jnp.zeros((8, width), jnp.float32))
        stats[me, :, columns(i)] = jnp.sum(total, axis=0, keepdims=True)

    def ring_copy(owner, step, i, way):
        which, c = groups[i]
        spot = pl.ds(pl.multiple_of(owner * rows + way * half, 16), half)
        piece = ready[which].at[spot, columns(c)]
        return pltpu.make_async_remote_copy(
            src_ref=piece, dst_ref=piece,
            send_sem=send_sem.at[way, step, i], recv_sem=recv_sem.at[way, step, i],
            device_id=(behind if way else ahead, side), device_id_type=MESH,
        )

    def owner_of(step, way):
        return node(step if way else -step)

    def send_own(i):
        which, c = groups[i]
        scale = scales[which][:, columns(c)]
        for way in range(2):

            def step(t, carry):
                at = pl.multiple_of(way * half + t * tile, 16)
                home = pl.multiple_of(me * rows + at, 16)
                ready[which][pl.ds(home, tile), columns(c)] = (
                    latest[which][pl.ds(at, tile), columns(c)] / scale
                ).astype(jnp.bfloat16)
                return carry

            lax.fori_loop(0, half // tile, step, 0)
            early(i, lambda: ring_copy(me, 0, i, way).start())

    def tell(part):
        for k in range(1, count):
            stat_copy(part, k).start()

    def finish(part):
        first, last = parts[part]
        for k in range(1, count):
            stat_copy(part, k).wait_recv()
        for i in range(first, last):
            which, c = groups[i]
            total = stats[0, :, columns(i)]
            for k in range(1, count):
                total = total + stats[k, :, columns(i)]
            scales[which][:, columns(c)] = jnp.sqrt(total)

    for part, (first, last) in enumerate(parts):
        for i in range(first, last):
            average(i)
        if part == 0:
            pl.semaphore_wait(barrier, count + across - 2)
        tell(part)
        if part == 0:
            for k in range(1, across):
                near_copy(k).start()
        else:
            finish(part - 1)
            for i in range(*parts[part - 1]):
                send_own(i)
    finish(len(parts) - 1)
    for i in range(*parts[-1]):
        send_own(i)
    for k in range(1, across):
        near_copy(k).wait_recv()
    for k in range(1, count):
        far_copy(k).start()

    def forward(step, carry):
        owners = owner_of(step, 0), owner_of(step, 1)
        for i in range(len(groups)):

            def pass_on():
                for way in range(2):
                    ring_copy(owners[way], step - 1, i, way).wait_recv()
                    ring_copy(owners[way], step, i, way).start()

            early(i, pass_on)
        return carry

    lax.fori_loop(1, count - 1, forward, 0)
    for i in range(len(groups)):

        def arrive():
            for way in range(2):
                ring_copy(owner_of(count - 1, way), count - 2, i, way).wait_recv()

        early(i, arrive)

    def drain(step, carry):
        for i in range(len(groups)):

            def leave():
                for way in range(2):
                    ring_copy(owner_of(step, way), step, i, way).wait_send()

            early(i, leave)
        return carry

    lax.fori_loop(0, count - 1, drain, 0)
    for k in range(1, count):
        for part in range(len(parts)):
            stat_copy(part, k).wait_send()
        far_copy(k).wait()
    for k in range(1, across):
        near_copy(k).wait_send()


def gather(arrays, norm_train, norm_step, count, across):
    rows = arrays[0].shape[0]
    wides = [a.shape[1] for a in arrays[::2]]
    half = rows // 2
    width = wides[1]
    tile = 112 if half % 112 == 0 else 16
    groups = [(1, 0)] + [(0, c) for c in range(wides[0] // width)] + [(2, 0)]
    n = len(groups)
    parts = [(0, 2), (2, 5), (5, n)]
    piece = norm_train.shape[0]
    hbm = pl.BlockSpec(memory_space=pl.ANY)
    vmem = pl.BlockSpec(memory_space=pltpu.VMEM)
    dma = pltpu.SemaphoreType.DMA
    return pl.pallas_call(
        functools.partial(gather_kernel, count, across, width, half, tile, groups, parts),
        in_specs=[hbm] * 6 + [vmem] * 2,
        out_specs=[vmem] * 10,
        out_shape=[pltpu.VMEM((count * rows, w), jnp.bfloat16) for w in wides]
        + [pltpu.VMEM((rows, w), jnp.float32) for w in wides]
        + [pltpu.VMEM((1, w), jnp.float32) for w in wides]
        + [pltpu.VMEM((count * across, 1, piece), jnp.float32)],
        scratch_shapes=[pltpu.VMEM(a.shape, jnp.float32) for a in arrays]
        + [
            pltpu.VMEM((count, 1, n * width), jnp.float32),
            dma((2, n)),
            dma((len(parts), count - 1)),
            dma((len(parts), count - 1)),
            dma((across - 1,)),
            dma((across - 1,)),
            dma((count - 1,)),
            dma((count - 1,)),
            dma((2, count - 1, n)),
            dma((2, count - 1, n)),
        ],
        compiler_params=pltpu.CompilerParams(
            collective_id=0, has_side_effects=True,
            vmem_limit_bytes=4 * sum(a.size for a in arrays) + 2**21,
        ),
    )(*arrays, norm_train.reshape(1, piece), norm_step.reshape(1, piece))


def pieces_of(source, target, sem, cuts):
    size = source.shape[0] // cuts
    copies = []
    for c in range(cuts):
        at = pl.ds(c * size, size)
        copies.append(pltpu.make_async_copy(source.at[at], target.at[at], sem.at[c]))
    return copies


def store_kernel(
    count, cuts,
    rk, rv, lq, lk, lv, scale_q, scale_k, scale_v, norm, rq,
    out_rk, out_rv, out_lq, out_lk, out_lv, out_sq, out_sk, out_sv, out_norm,
    sem, own_sem,
):
    late = lax.rem(lax.axis_index("width"), 2) == 0
    copies = []
    pairs = ((lq, out_lq), (rk, out_rk), (lk, out_lk), (lv, out_lv))
    for i, (source, target) in enumerate(pairs):
        copies += pieces_of(source, target, sem.at[i], cuts)
    for copy in copies:
        copy.start()
    size = rv.shape[0] // count
    at = pl.ds(pl.multiple_of(lax.axis_index("zero") * size, 16), size)
    own = pltpu.make_async_copy(rv.at[at], out_rv.at[at], own_sem)
    whole = pieces_of(rv, out_rv, sem.at[len(pairs)], cuts)

    @pl.when(late)
    def _():
        own.start()

    @pl.when(jnp.logical_not(late))
    def _():
        for copy in whole:
            copy.start()

    for source, target in ((scale_q, out_sq), (scale_k, out_sk), (scale_v, out_sv)):
        target[...] = source[0, :]
    out_norm[...] = norm[...].astype(jnp.bfloat16)
    for copy in copies:
        copy.wait()

    @pl.when(late)
    def _():
        own.wait()

    @pl.when(jnp.logical_not(late))
    def _():
        for copy in whole:
            copy.wait()


def store(arrays, count):
    cuts = 8
    hbm = pl.BlockSpec(memory_space=pltpu.HBM)
    vmem = pl.BlockSpec(memory_space=pltpu.VMEM)
    return pl.pallas_call(
        functools.partial(store_kernel, count, cuts),
        in_specs=[vmem] * (len(arrays) - 1) + [hbm],
        out_specs=[hbm] * 5 + [vmem] * 4,
        out_shape=[jax.ShapeDtypeStruct(a.shape, a.dtype) for a in arrays[:5]]
        + [jax.ShapeDtypeStruct((a.shape[1],), a.dtype) for a in arrays[5:8]]
        + [jax.ShapeDtypeStruct(arrays[8].shape, jnp.bfloat16)],
        scratch_shapes=[pltpu.SemaphoreType.DMA((5, cuts)), pltpu.SemaphoreType.DMA],
        compiler_params=pltpu.CompilerParams(vmem_limit_bytes=2 * arrays[-1].size + 2**20),
    )(*arrays)


def store_one_kernel(cuts, source, target, sem):
    copies = pieces_of(source, target, sem, cuts)
    for copy in copies:
        copy.start()
    for copy in copies:
        copy.wait()


def store_one(array):
    cuts = 8
    return pl.pallas_call(
        functools.partial(store_one_kernel, cuts),
        in_specs=[pl.BlockSpec(memory_space=pltpu.VMEM)],
        out_specs=pl.BlockSpec(memory_space=pltpu.HBM),
        out_shape=jax.ShapeDtypeStruct(array.shape, array.dtype),
        scratch_shapes=[pltpu.SemaphoreType.DMA((cuts,))],
        compiler_params=pltpu.CompilerParams(vmem_limit_bytes=2**20),
    )(array)


def late_kernel(count, half, cuts, own, after, rv, load_sem, send_sem, recv_sem):
    me, node = ring_of(count)
    side = lax.axis_index("width")
    ahead, behind = node(1), node(-1)
    size = half // cuts

    def ring_copy(owner, step, i, way):
        spot = pl.ds(pl.multiple_of(owner * 2 * half + way * half + i * size, 16), size)
        piece = rv.at[spot]
        return pltpu.make_async_remote_copy(
            src_ref=piece, dst_ref=piece,
            send_sem=send_sem.at[way, step, i], recv_sem=recv_sem.at[way, step, i],
            device_id=(behind if way else ahead, side), device_id_type=MESH,
        )

    def owner_of(step, way):
        return node(step if way else -step)

    @pl.when(lax.rem(side, 2) == 0)
    def _():
        barrier = pltpu.get_barrier_semaphore()
        for other in (ahead, behind):
            pl.semaphore_signal(barrier, inc=1, device_id=(other, side), device_id_type=MESH)
        at = pl.ds(pl.multiple_of(me * 2 * half, 16), 2 * half)
        load = pltpu.make_async_copy(own.at[at], rv.at[at], load_sem)
        load.start()
        load.wait()
        pl.semaphore_wait(barrier, 2)
        for i in range(cuts):
            for way in range(2):
                ring_copy(me, 0, i, way).start()

        def forward(step, carry):
            for i in range(cuts):
                for way in range(2):
                    ring_copy(owner_of(step, way), step - 1, i, way).wait_recv()
                    ring_copy(owner_of(step, way), step, i, way).start()
            return carry

        lax.fori_loop(1, count - 1, forward, 0)
        for i in range(cuts):
            for way in range(2):
                ring_copy(owner_of(count - 1, way), count - 2, i, way).wait_recv()

        def drain(step, carry):
            for i in range(cuts):
                for way in range(2):
                    ring_copy(owner_of(step, way), step, i, way).wait_send()
            return carry

        lax.fori_loop(0, count - 1, drain, 0)


def gather_late(own, after, count):
    half = own.shape[0] // count // 2
    cuts = 7 if half % 112 == 0 else 1
    hbm = pl.BlockSpec(memory_space=pltpu.HBM)
    dma = pltpu.SemaphoreType.DMA
    return pl.pallas_call(
        functools.partial(late_kernel, count, half, cuts),
        in_specs=[hbm, hbm],
        out_specs=pl.BlockSpec(memory_space=pltpu.VMEM),
        out_shape=pltpu.VMEM(own.shape, own.dtype),
        scratch_shapes=[dma, dma((2, count - 1, cuts)), dma((2, count - 1, cuts))],
        compiler_params=pltpu.CompilerParams(
            collective_id=1, has_side_effects=True, vmem_limit_bytes=60 * 2**20
        ),
    )(own, after)


def store_late_kernel(cuts, rv, start, out, sem):
    @pl.when(lax.rem(lax.axis_index("width"), 2) == 0)
    def _():
        copies = pieces_of(rv, out, sem, cuts)
        for copy in copies:
            copy.start()
        for copy in copies:
            copy.wait()


def store_late(rv, start):
    cuts = 8
    hbm = pl.BlockSpec(memory_space=pltpu.HBM)
    return pl.pallas_call(
        functools.partial(store_late_kernel, cuts),
        in_specs=[pl.BlockSpec(memory_space=pltpu.VMEM), hbm],
        out_specs=hbm,
        out_shape=jax.ShapeDtypeStruct(start.shape, start.dtype),
        scratch_shapes=[pltpu.SemaphoreType.DMA((cuts,))],
        input_output_aliases={1: 0},
        compiler_params=pltpu.CompilerParams(vmem_limit_bytes=2**20),
    )(rv, start)


def solution(mesh):
    count, across = mesh.shape["zero"], mesh.shape["width"]

    def body(
        train_query, slow_query, train_key, slow_key, train_value, slow_value, norm_train, norm_step
    ):
        arrays = gather(
            (train_query, slow_query, train_key, slow_key, train_value, slow_value),
            norm_train, norm_step, count, across,
        )
        rq = store_one(arrays[0])
        rk, rv, lq, lk, lv, *scales, norm = store((*arrays[1:], rq), count)
        serve_norm = norm.reshape(-1)
        rv = store_late(gather_late(rv, serve_norm, count), rv)
        return (rq, rk, rv, *scales, serve_norm, lq, lk, lv)

    in_specs = (P("zero", "width"),) * 6 + (P(("zero", "width")),) * 2
    out_specs = (
        (P(None, "width"),) * 3 + (P("width"),) * 3 + (P(),) + (P("zero", "width"),) * 3
    )
    return jax.shard_map(body, mesh=mesh, in_specs=in_specs, out_specs=out_specs, check_vma=False)
```

time: 354 us -> 336 us (0.949)
  local copies, waits for them, and re-layouts: 11.8 us -> 0.7 us
  Pallas kernels: 341 us -> 334 us
    pallas_call x1, Pallas kernels: 326 us -> 292 us  [gather(): pl.pallas_call(functools.partial(gather_kernel, count, across, width, hal...]
    pallas_call x2 -> x4, Pallas kernels: 14.9 us -> 42 us  [the longest x1 25.9 us: gather_late(): pl.pallas_call(functools.partial(late_kernel, count, half, cuts), in_spec...]
    unnamed x14 -> x0, local copies, waits for them, and re-layouts: 11.1 us -> none
where the time goes in v1:
time: 336 us
  Pallas kernels  334 us (99%)
    pallas_call x1, Pallas kernels, gather(): pl.pallas_call(functools.partial(gather_kernel, count, across, width, hal...  292 us
    pallas_call x1, Pallas kernels, gather_late(): pl.pallas_call(functools.partial(late_kernel, count, half, cuts), in_spec...  25.9 us
    pallas_call x1, Pallas kernels, store_one(): pl.pallas_call(functools.partial(store_one_kernel, cuts), in_specs=[pl.Bl...  8.7 us

profile of v1, /device:TPU:0, one launch (start us, length us, event | category | flops | bytes accessed | tf_op | source)
XLA Modules:
  0.0 335.8 jit_solution(16571030881520542602)
XLA Ops:
  0.6 292.3 %shard_map.159 = (bf16[7168,1792]{1,0:T(8,128)(2,1)S(1)}, bf16[7168,256]{1,0:T(8,128)(2,1)S(1)}, bf16[7168,256]{1,0:T(8,128)(2,1)S(1)}, f32[896,1792]{1,0:T(8,12...) custom-call(f32[896,1792]{1,0:T(8,128)} %tq.1, ...), custom_call_target="tpu_custom_call" | custom-call | tf_op jit(solution)/shard_map/pallas_call | solution.py:263
  293.0 8.7 %shard_map.160.rq = bf16[7168,1792]{1,0:T(8,128)(2,1)} custom-call(bf16[7168,1792]{1,0:T(8,128)(2,1)S(1)} %get-tuple-element.29.source), custom_call_target="tpu_custom_call" | custom-call | tf_op jit(solution)/shard_map/pallas_call | solution.py:369
  301.7 5.5 %shard_map.161 = (bf16[7168,256]{1,0:T(8,128)(2,1)}, bf16[7168,256]{1,0:T(8,128)(2,1)}, f32[896,1792]{1,0:T(8,128)}, f32[896,256]{1,0:T(8,128)}, f32[896,256]{1,...) custom-call(bf16[7168,256]{1,0:T(8,128)(2,1)S(1)} %get-tuple-element.30.rk, ...), custom_call_target="tpu_custom_call" | custom-call | tf_op jit(solution)/shard_map/pallas_call | solution.py:347
  307.2 0.1 reduce
  307.3 0.7 reshape.31.after
  308.0 25.9 %shard_map.162.rv = bf16[7168,256]{1,0:T(8,128)(2,1)S(1)} custom-call(bf16[7168,256]{1,0:T(8,128)(2,1)} %get-tuple-element.40.own.start, bf16[7168]{0:T(1024)(128)(2,1)} %reshape.31.after), custom_call_target="tpu_custom_call" | custom-call | tf_op jit(solution)/shard_map/pallas_call | solution.py:437
  333.9 1.9 shard_map.163

commit v2 on v1

--- a/solution.py
+++ b/solution.py
@@ -54,7 +54,7 @@
 
 
 def gather_kernel(
-    count, across, width, half, tile, groups, parts,
+    count, across, width, half, tile, groups, parts, pieces,
     tq, sq, tk, sk, tv, sv, norm_train, norm_step,
     rq, rk, rv, lq, lk, lv, scale_q, scale_k, scale_v, norm_all,
     itq, isq, itk, isk, itv, isv, stats,
@@ -72,8 +72,8 @@
     def columns(c):
         return pl.ds(c * width, width)
 
-    def early(i, action):
-        if groups[i][0] == 2:
+    def allowed(p, action):
+        if pieces[p][3]:
             pl.when(jnp.logical_not(late))(action)
         else:
             action()
@@ -142,13 +142,14 @@
         total = lax.fori_loop(0, rows // tile, step, jnp.zeros((8, width), jnp.float32))
         stats[me, :, columns(i)] = jnp.sum(total, axis=0, keepdims=True)
 
-    def ring_copy(owner, step, i, way):
+    def ring_copy(owner, step, p, way):
+        i, first, size, _ = pieces[p]
         which, c = groups[i]
-        spot = pl.ds(pl.multiple_of(owner * rows + way * half, 16), half)
+        spot = pl.ds(pl.multiple_of(owner * rows + way * half + first, 16), size)
         piece = ready[which].at[spot, columns(c)]
         return pltpu.make_async_remote_copy(
             src_ref=piece, dst_ref=piece,
-            send_sem=send_sem.at[way, step, i], recv_sem=recv_sem.at[way, step, i],
+            send_sem=send_sem.at[way, lax.rem(step, 2), p], recv_sem=recv_sem.at[way, step, p],
             device_id=(behind if way else ahead, side), device_id_type=MESH,
         )
 
@@ -169,7 +170,9 @@
                 return carry
 
             lax.fori_loop(0, half // tile, step, 0)
-            early(i, lambda: ring_copy(me, 0, i, way).start())
+            for p in range(len(pieces)):
+                if pieces[p][0] == i:
+                    allowed(p, lambda: ring_copy(me, 0, p, way).start())
 
     def tell(part):
         for k in range(1, count):
@@ -207,44 +210,47 @@
     for k in range(1, count):
         far_copy(k).start()
 
+    def leave(step):
+        for p in range(len(pieces)):
+
+            def left():
+                for way in range(2):
+                    ring_copy(owner_of(step, way), step, p, way).wait_send()
+
+            allowed(p, left)
+
     def forward(step, carry):
         owners = owner_of(step, 0), owner_of(step, 1)
-        for i in range(len(groups)):
+        for p in range(len(pieces)):
 
             def pass_on():
                 for way in range(2):
-                    ring_copy(owners[way], step - 1, i, way).wait_recv()
-                    ring_copy(owners[way], step, i, way).start()
-
-            early(i, pass_on)
+                    ring_copy(owners[way], step - 1, p, way).wait_recv()
+                    ring_copy(owners[way], step, p, way).start()
+
+            allowed(p, pass_on)
+        leave(step - 1)
         return carry
 
     lax.fori_loop(1, count - 1, forward, 0)
-    for i in range(len(groups)):
-
-        def arrive():
-            for way in range(2):
-                ring_copy(owner_of(count - 1, way), count - 2, i, way).wait_recv()
-
-        early(i, arrive)
-
-    def drain(step, carry):
-        for i in range(len(groups)):
-
-            def leave():
-                for way in range(2):
-                    ring_copy(owner_of(step, way), step, i, way).wait_send()
-
-            early(i, leave)
-        return carry
-
-    lax.fori_loop(0, count - 1, drain, 0)
     for k in range(1, count):
         for part in range(len(parts)):
             stat_copy(part, k).wait_send()
         far_copy(k).wait()
     for k in range(1, across):
         near_copy(k).wait_send()
+    for p in range(len(pieces)):
+
+        def arrive():
+            for way in range(2):
+                ring_copy(owner_of(count - 1, way), count - 2, p, way).wait_recv()
+
+        allowed(p, arrive)
+    leave(count - 2)
+
+
+def cut_of(half):
+    return half // 32 * 16
 
 
 def gather(arrays, norm_train, norm_step, count, across):
@@ -255,13 +261,16 @@
     tile = 112 if half % 112 == 0 else 16
     groups = [(1, 0)] + [(0, c) for c in range(wides[0] // width)] + [(2, 0)]
     n = len(groups)
+    cut = cut_of(half)
+    pieces = [(i, 0, half, False) for i in range(1, n - 1)]
+    pieces = [(0, 0, cut, False), (0, cut, half - cut, True)] + pieces + [(n - 1, 0, half, True)]
     parts = [(0, 2), (2, 5), (5, n)]
     piece = norm_train.shape[0]
     hbm = pl.BlockSpec(memory_space=pl.ANY)
     vmem = pl.BlockSpec(memory_space=pltpu.VMEM)
     dma = pltpu.SemaphoreType.DMA
     return pl.pallas_call(
-        functools.partial(gather_kernel, count, across, width, half, tile, groups, parts),
+        functools.partial(gather_kernel, count, across, width, half, tile, groups, parts, pieces),
         in_specs=[hbm] * 6 + [vmem] * 2,
         out_specs=[vmem] * 10,
         out_shape=[pltpu.VMEM((count * rows, w), jnp.bfloat16) for w in wides]
@@ -278,8 +287,8 @@
             dma((across - 1,)),
             dma((count - 1,)),
             dma((count - 1,)),
-            dma((2, count - 1, n)),
-            dma((2, count - 1, n)),
+            dma((2, 2, len(pieces))),
+            dma((2, count - 1, len(pieces))),
         ],
         compiler_params=pltpu.CompilerParams(
             collective_id=0, has_side_effects=True,
@@ -297,51 +306,74 @@
     return copies
 
 
+def key_pieces(count, rows, late, small):
+    half = rows // 2
+    cut = cut_of(half)
+    size = half - cut if late else cut
+    pieces = []
+    for owner in range(count):
+        for way in range(2):
+            spot = pl.ds(owner * rows + way * half + (cut if late else 0), size)
+            pieces.append((pl.ds((owner * 2 + way) * size, size) if small else spot, spot))
+    return pieces
+
+
 def store_kernel(
     count, cuts,
     rk, rv, lq, lk, lv, scale_q, scale_k, scale_v, norm, rq,
     out_rk, out_rv, out_lq, out_lk, out_lv, out_sq, out_sk, out_sv, out_norm,
-    sem, own_sem,
+    sem, key_sem, own_sem,
 ):
     late = lax.rem(lax.axis_index("width"), 2) == 0
-    copies = []
-    pairs = ((lq, out_lq), (rk, out_rk), (lk, out_lk), (lv, out_lv))
-    for i, (source, target) in enumerate(pairs):
-        copies += pieces_of(source, target, sem.at[i], cuts)
-    for copy in copies:
+    rows = rv.shape[0] // count
+    base = lax.axis_index("zero") * rows
+    half = rows // 2
+    cut = cut_of(half)
+    both, last, first = [], [], []
+    for i, (source, target) in enumerate(((lq, out_lq), (lk, out_lk), (lv, out_lv))):
+        both += pieces_of(source, target, sem.at[i], cuts)
+    first += pieces_of(rk, out_rk, sem.at[3], cuts) + pieces_of(rv, out_rv, sem.at[4], cuts)
+    for i, (_, at) in enumerate(key_pieces(count, rows, False, False)):
+        last.append(pltpu.make_async_copy(rk.at[at], out_rk.at[at], key_sem.at[i]))
+    at = pl.ds(pl.multiple_of(base, 16), rows)
+    last.append(pltpu.make_async_copy(rv.at[at], out_rv.at[at], own_sem.at[0]))
+    for way in range(2):
+        at = pl.ds(pl.multiple_of(base + way * half + cut, 16), half - cut)
+        last.append(pltpu.make_async_copy(rk.at[at], out_rk.at[at], own_sem.at[1 + way]))
+
+    for copy in both:
         copy.start()
-    size = rv.shape[0] // count
-    at = pl.ds(pl.multiple_of(lax.axis_index("zero") * size, 16), size)
-    own = pltpu.make_async_copy(rv.at[at], out_rv.at[at], own_sem)
-    whole = pieces_of(rv, out_rv, sem.at[len(pairs)], cuts)
 
     @pl.when(late)
     def _():
-        own.start()
+        for copy in last:
+            copy.start()
 
     @pl.when(jnp.logical_not(late))
     def _():
-        for copy in whole:
+        for copy in first:
             copy.start()
 
     for source, target in ((scale_q, out_sq), (scale_k, out_sk), (scale_v, out_sv)):
         target[...] = source[0, :]
     out_norm[...] = norm[...].astype(jnp.bfloat16)
-    for copy in copies:
+    for copy in both:
         copy.wait()
 
     @pl.when(late)
     def _():
-        own.wait()
+        for copy in last:
+            copy.wait()
 
     @pl.when(jnp.logical_not(late))
     def _():
-        for copy in whole:
+        for copy in first:
             copy.wait()
 
 
 def store(arrays, count):
     cuts = 8
+    dma = pltpu.SemaphoreType.DMA
     hbm = pl.BlockSpec(memory_space=pltpu.HBM)
     vmem = pl.BlockSpec(memory_space=pltpu.VMEM)
     return pl.pallas_call(
@@ -351,7 +383,7 @@
         out_shape=[jax.ShapeDtypeStruct(a.shape, a.dtype) for a in arrays[:5]]
         + [jax.ShapeDtypeStruct((a.shape[1],), a.dtype) for a in arrays[5:8]]
         + [jax.ShapeDtypeStruct(arrays[8].shape, jnp.bfloat16)],
-        scratch_shapes=[pltpu.SemaphoreType.DMA((5, cuts)), pltpu.SemaphoreType.DMA],
+        scratch_shapes=[dma((5, cuts)), dma((2 * count,)), dma((3,))],
         compiler_params=pltpu.CompilerParams(vmem_limit_bytes=2 * arrays[-1].size + 2**20),
     )(*arrays)
 
@@ -376,98 +408,117 @@
     )(array)
 
 
-def late_kernel(count, half, cuts, own, after, rv, load_sem, send_sem, recv_sem):
+def late_kernel(count, half, tile, own_k, own_v, after, rk, rv, load_sem, send_sem, recv_sem):
     me, node = ring_of(count)
     side = lax.axis_index("width")
     ahead, behind = node(1), node(-1)
-    size = half // cuts
-
-    def ring_copy(owner, step, i, way):
-        spot = pl.ds(pl.multiple_of(owner * 2 * half + way * half + i * size, 16), size)
-        piece = rv.at[spot]
+    cut = cut_of(half)
+    rest = half - cut
+    pieces = [(rk, rest, t * tile) for t in range(rest // tile)]
+    pieces += [(rv, half, t * tile) for t in range(half // tile)]
+
+    def ring_copy(owner, step, p, way):
+        ref, size, first = pieces[p]
+        piece = ref.at[pl.ds(pl.multiple_of((owner * 2 + way) * size + first, 16), tile)]
         return pltpu.make_async_remote_copy(
             src_ref=piece, dst_ref=piece,
-            send_sem=send_sem.at[way, step, i], recv_sem=recv_sem.at[way, step, i],
+            send_sem=send_sem.at[way, lax.rem(step, 2), p], recv_sem=recv_sem.at[way, step, p],
             device_id=(behind if way else ahead, side), device_id_type=MESH,
         )
 
     def owner_of(step, way):
         return node(step if way else -step)
+
+    def leave(step):
+        for p in range(len(pieces)):
+            for way in range(2):
+                ring_copy(owner_of(step, way), step, p, way).wait_send()
 
     @pl.when(lax.rem(side, 2) == 0)
     def _():
         barrier = pltpu.get_barrier_semaphore()
         for other in (ahead, behind):
             pl.semaphore_signal(barrier, inc=1, device_id=(other, side), device_id_type=MESH)
-        at = pl.ds(pl.multiple_of(me * 2 * half, 16), 2 * half)
-        load = pltpu.make_async_copy(own.at[at], rv.at[at], load_sem)
-        load.start()
-        load.wait()
+        loads = []
+        for way in range(2):
+            there = pl.ds(pl.multiple_of((me * 2 + way) * half + cut, 16), rest)
+            here = pl.ds(pl.multiple_of((me * 2 + way) * rest, 16), rest)
+            loads.append(pltpu.make_async_copy(own_k.at[there], rk.at[here], load_sem.at[0, way]))
+            at = pl.ds(pl.multiple_of((me * 2 + way) * half, 16), half)
+            loads.append(pltpu.make_async_copy(own_v.at[at], rv.at[at], load_sem.at[1, way]))
+        for load in loads:
+            load.start()
+        for load in loads:
+            load.wait()
         pl.semaphore_wait(barrier, 2)
-        for i in range(cuts):
+        for p in range(len(pieces)):
             for way in range(2):
-                ring_copy(me, 0, i, way).start()
+                ring_copy(me, 0, p, way).start()
 
         def forward(step, carry):
-            for i in range(cuts):
+            for p in range(len(pieces)):
                 for way in range(2):
-                    ring_copy(owner_of(step, way), step - 1, i, way).wait_recv()
-                    ring_copy(owner_of(step, way), step, i, way).start()
+                    ring_copy(owner_of(step, way), step - 1, p, way).wait_recv()
+                    ring_copy(owner_of(step, way), step, p, way).start()
+            leave(step - 1)
             return carry
 
         lax.fori_loop(1, count - 1, forward, 0)
-        for i in range(cuts):
+        for p in range(len(pieces)):
             for way in range(2):
-                ring_copy(owner_of(count - 1, way), count - 2, i, way).wait_recv()
-
-        def drain(step, carry):
-            for i in range(cuts):
-                for way in range(2):
-                    ring_copy(owner_of(step, way), step, i, way).wait_send()
-            return carry
-
-        lax.fori_loop(0, count - 1, drain, 0)
-
-
-def gather_late(own, after, count):
-    half = own.shape[0] // count // 2
-    cuts = 7 if half % 112 == 0 else 1
+                ring_copy(owner_of(count - 1, way), count - 2, p, way).wait_recv()
+        leave(count - 2)
+
+
+def gather_late(own_k, own_v, after, count):
+    half = own_k.shape[0] // count // 2
+    rest = half - cut_of(half)
+    tile = 112 if rest % 112 == 0 and half % 112 == 0 else 16
+    n = (rest + half) // tile
     hbm = pl.BlockSpec(memory_space=pltpu.HBM)
+    vmem = pl.BlockSpec(memory_space=pltpu.VMEM)
     dma = pltpu.SemaphoreType.DMA
     return pl.pallas_call(
-        functools.partial(late_kernel, count, half, cuts),
-        in_specs=[hbm, hbm],
-        out_specs=pl.BlockSpec(memory_space=pltpu.VMEM),
-        out_shape=pltpu.VMEM(own.shape, own.dtype),
-        scratch_shapes=[dma, dma((2, count - 1, cuts)), dma((2, count - 1, cuts))],
+        functools.partial(late_kernel, count, half, tile),
+        in_specs=[hbm] * 3,
+        out_specs=[vmem] * 2,
+        out_shape=[
+            pltpu.VMEM((2 * count * rest, own_k.shape[1]), own_k.dtype),
+            pltpu.VMEM(own_v.shape, own_v.dtype),
+        ],
+        scratch_shapes=[dma((2, 2)), dma((2, 2, n)), dma((2, count - 1, n))],
         compiler_params=pltpu.CompilerParams(
-            collective_id=1, has_side_effects=True, vmem_limit_bytes=60 * 2**20
+            collective_id=1, has_side_effects=True, vmem_limit_bytes=56 * 2**20
         ),
-    )(own, after)
-
-
-def store_late_kernel(cuts, rv, start, out, sem):
+    )(own_k, own_v, after)
+
+
+def store_late_kernel(count, cuts, rk, rv, start_k, start_v, out_k, out_v, sem, key_sem):
     @pl.when(lax.rem(lax.axis_index("width"), 2) == 0)
     def _():
-        copies = pieces_of(rv, out, sem, cuts)
+        copies = pieces_of(rv, out_v, sem, cuts)
+        for i, (here, there) in enumerate(key_pieces(count, rv.shape[0] // count, True, True)):
+            copies.append(pltpu.make_async_copy(rk.at[here], out_k.at[there], key_sem.at[i]))
         for copy in copies:
             copy.start()
         for copy in copies:
             copy.wait()
 
 
-def store_late(rv, start):
+def store_late(rk, rv, start_k, start_v, count):
     cuts = 8
     hbm = pl.BlockSpec(memory_space=pltpu.HBM)
+    vmem = pl.BlockSpec(memory_space=pltpu.VMEM)
+    dma = pltpu.SemaphoreType.DMA
     return pl.pallas_call(
-        functools.partial(store_late_kernel, cuts),
-        in_specs=[pl.BlockSpec(memory_space=pltpu.VMEM), hbm],
-        out_specs=hbm,
-        out_shape=jax.ShapeDtypeStruct(start.shape, start.dtype),
-        scratch_shapes=[pltpu.SemaphoreType.DMA((cuts,))],
-        input_output_aliases={1: 0},
-        compiler_params=pltpu.CompilerParams(vmem_limit_bytes=2**20),
-    )(rv, start)
+        functools.partial(store_late_kernel, count, cuts),
+        in_specs=[vmem] * 2 + [hbm] * 2,
+        out_specs=[hbm] * 2,
+        out_shape=[jax.ShapeDtypeStruct(a.shape, a.dtype) for a in (start_k, start_v)],
+        scratch_shapes=[dma((cuts,)), dma((2 * count,))],
+        input_output_aliases={2: 0, 3: 1},
+        compiler_params=pltpu.CompilerParams(vmem_limit_bytes=40 * 2**20),
+    )(rk, rv, start_k, start_v)
 
 
 def solution(mesh):
@@ -483,7 +534,7 @@
         rq = store_one(arrays[0])
         rk, rv, lq, lk, lv, *scales, norm = store((*arrays[1:], rq), count)
         serve_norm = norm.reshape(-1)
-        rv = store_late(gather_late(rv, serve_norm, count), rv)
+        rk, rv = store_late(*gather_late(rk, rv, serve_norm, count), rk, rv, count)
         return (rq, rk, rv, *scales, serve_norm, lq, lk, lv)
 
     in_specs = (P("zero", "width"),) * 6 + (P(("zero", "width")),) * 2

time: 336 us -> 326 us (0.970)
  Pallas kernels: 334 us -> 325 us
    pallas_call x1, Pallas kernels: 292 us -> 274 us  [gather(): pl.pallas_call(functools.partial(gather_kernel, count, across, width, hal...]
    pallas_call x2, Pallas kernels: 27.9 us -> 36.6 us  [the longest x1 34 us: gather_late(): pl.pallas_call(functools.partial(late_kernel, count, half, tile), in_spec...]
where the time goes in v2:
time: 326 us
  Pallas kernels  325 us (100%)
    pallas_call x1, Pallas kernels, gather(): pl.pallas_call(functools.partial(gather_kernel, count, across, width, hal...  274 us
    pallas_call x1, Pallas kernels, gather_late(): pl.pallas_call(functools.partial(late_kernel, count, half, tile), in_spec...  34 us
    pallas_call x1, Pallas kernels, store_one(): pl.pallas_call(functools.partial(store_one_kernel, cuts), in_specs=[pl.Bl...  8.7 us

profile of v2, /device:TPU:0, one launch (start us, length us, event | category | flops | bytes accessed | tf_op | source)
XLA Modules:
  0.0 326.2 jit_solution(14997411617477145840)
XLA Ops:
  0.6 274.3 %shard_map.159 = (bf16[7168,1792]{1,0:T(8,128)(2,1)S(1)}, bf16[7168,256]{1,0:T(8,128)(2,1)S(1)}, bf16[7168,256]{1,0:T(8,128)(2,1)S(1)}, f32[896,1792]{1,0:T(8,12...) custom-call(f32[896,1792]{1,0:T(8,128)} %tq.1, ...), custom_call_target="tpu_custom_call" | custom-call | tf_op jit(solution)/shard_map/pallas_call | solution.py:272
  274.9 8.7 %shard_map.160.rq = bf16[7168,1792]{1,0:T(8,128)(2,1)} custom-call(bf16[7168,1792]{1,0:T(8,128)(2,1)S(1)} %get-tuple-element.33.source), custom_call_target="tpu_custom_call" | custom-call | tf_op jit(solution)/shard_map/pallas_call | solution.py:401
  283.6 5.1 %shard_map.161 = (bf16[7168,256]{1,0:T(8,128)(2,1)}, bf16[7168,256]{1,0:T(8,128)(2,1)}, f32[896,1792]{1,0:T(8,128)}, f32[896,256]{1,0:T(8,128)}, f32[896,256]{1,...) custom-call(bf16[7168,256]{1,0:T(8,128)(2,1)S(1)} %get-tuple-element.34.rk, ...), custom_call_target="tpu_custom_call" | custom-call | tf_op jit(solution)/shard_map/pallas_call | solution.py:379
  288.8 0.1 reduce
  288.9 0.7 reshape.31.after
  289.6 34.0 %shard_map.162 = (bf16[3584,256]{1,0:T(8,128)(2,1)S(1)}, bf16[7168,256]{1,0:T(8,128)(2,1)S(1)}) custom-call(bf16[7168,256]{1,0:T(8,128)(2,1)} %get-tuple-element.43.own_k.start_k, bf16[7168,256]{1,0:T(8,128)(2,1)} %get-tuple-element.44.own_v.start_v, bf16[7168]{0:T(1024)(128)(2,1)} %reshape.31.after), custom_call_target="tpu_custom_call" | custom-call | tf_op jit(solution)/shard_map/pallas_call | solution.py:481
  323.5 2.6 shard_map.163

commit v3 on v2

--- a/solution.py
+++ b/solution.py
@@ -54,26 +54,27 @@
 
 
 def gather_kernel(
-    count, across, width, half, tile, groups, parts, pieces,
+    count, across, width, half, tile, raw_rows, parts, batches, pieces,
     tq, sq, tk, sk, tv, sv, norm_train, norm_step,
     rq, rk, rv, lq, lk, lv, scale_q, scale_k, scale_v, norm_all,
-    itq, isq, itk, isk, itv, isv, stats,
-    load_sem, stat_send, stat_recv, near_send, near_recv, far_send, far_recv,
+    itq, isq, itk, isk, itv, isv, in_train, in_step, stats, raw,
+    load_sem, norm_sem, stat_send, stat_recv, near_sem, far_sem, raw_send, raw_recv,
     send_sem, recv_sem,
 ):
     me, node = ring_of(count)
     side = lax.axis_index("width")
-    late = lax.rem(side, 2) == 0
+    late = lax.rem(side, 2) == 1
     ahead, behind = node(1), node(-1)
     rows = 2 * half
     trains, slows = ((tq, itq), (tk, itk), (tv, itv)), ((sq, isq), (sk, isk), (sv, isv))
     latest, ready, scales = (lq, lk, lv), (rq, rk, rv), (scale_q, scale_k, scale_v)
-
-    def columns(c):
-        return pl.ds(c * width, width)
+    groups = [group for part in parts for group in part]
+
+    def columns(c, n=1):
+        return pl.ds(c * width, n * width)
 
     def allowed(p, action):
-        if pieces[p][3]:
+        if pieces[p][5]:
             pl.when(jnp.logical_not(late))(action)
         else:
             action()
@@ -89,46 +90,62 @@
         )
 
     loads = []
-    for i, (which, c) in enumerate(groups):
-        pair = []
+    for i, (_, which, c, n) in enumerate(batches):
         for j, arrays in enumerate((trains, slows)):
             far, near = arrays[which]
-            pair.append(
-                pltpu.make_async_copy(far.at[:, columns(c)], near.at[:, columns(c)], load_sem.at[j, i])
+            loads.append(
+                pltpu.make_async_copy(
+                    far.at[:, columns(c, n)], near.at[:, columns(c, n)], load_sem.at[i, j]
+                )
             )
-            pair[-1].start()
-        loads.append(pair)
+            loads[-1].start()
+    norms = [
+        pltpu.make_async_copy(far, near, norm_sem.at[j])
+        for j, (far, near) in enumerate(((norm_train, in_train), (norm_step, in_step)))
+    ]
+    for load in norms:
+        load.start()
     mine = me * across + side
-    norm_all[mine] = norm_train[...] + norm_step[...]
+
+    def part_columns(part):
+        first = groups.index(parts[part][0])
+        return columns(first, len(parts[part]))
 
     def stat_copy(part, k):
-        first, last = parts[part]
-        piece = stats.at[me, :, pl.ds(first * width, (last - first) * width)]
+        piece = stats.at[me, :, part_columns(part)]
         return pltpu.make_async_remote_copy(
-            src_ref=piece, dst_ref=piece,
-            send_sem=stat_send.at[part, k - 1], recv_sem=stat_recv.at[part, k - 1],
+            src_ref=piece, dst_ref=piece, send_sem=stat_send.at[0], recv_sem=stat_recv.at[part],
             device_id=(lax.rem(me + k, count), side), device_id_type=MESH,
         )
 
-    def near_copy(k):
+    def all_stats(part=None):
+        piece = stats.at[pl.ds(0, count - 1)]
+        if part is not None:
+            piece = stats.at[pl.ds(0, count - 1), :, part_columns(part)]
         return pltpu.make_async_remote_copy(
-            src_ref=norm_all.at[mine], dst_ref=norm_all.at[mine],
-            send_sem=near_send.at[k - 1], recv_sem=near_recv.at[k - 1],
-            device_id=(me, lax.rem(side + k, across)), device_id_type=MESH,
-        )
-
-    def far_copy(k):
-        at = pl.ds(me * across, across)
+            src_ref=piece, dst_ref=piece, send_sem=stat_send.at[0],
+            recv_sem=stat_recv.at[part or 0], device_id=(ahead, side), device_id_type=MESH,
+        )
+
+    def near_copy(at, k=1):
         return pltpu.make_async_remote_copy(
             src_ref=norm_all.at[at], dst_ref=norm_all.at[at],
-            send_sem=far_send.at[k - 1], recv_sem=far_recv.at[k - 1],
+            send_sem=near_sem.at[0], recv_sem=near_sem.at[1],
+            device_id=(me, lax.rem(side + k, across)), device_id_type=MESH,
+        )
+
+    def far_copy(at, k=1):
+        return pltpu.make_async_remote_copy(
+            src_ref=norm_all.at[at], dst_ref=norm_all.at[at],
+            send_sem=far_sem.at[0], recv_sem=far_sem.at[1],
             device_id=(lax.rem(me + k, count), side), device_id_type=MESH,
         )
+
+    all_near = near_copy(pl.ds(0, across - 1))
+    all_far = far_copy(pl.ds(0, (count - 1) * across))
 
     def average(i):
         which, c = groups[i]
-        for load in loads[i]:
-            load.wait()
 
         def step(t, total):
             at = pl.ds(pl.multiple_of(t * tile, 16), tile)
@@ -142,36 +159,54 @@
         total = lax.fori_loop(0, rows // tile, step, jnp.zeros((8, width), jnp.float32))
         stats[me, :, columns(i)] = jnp.sum(total, axis=0, keepdims=True)
 
+    def averages(part):
+        for i, batch in enumerate(batches):
+            if batch[0] == part:
+                loads[2 * i].wait()
+                loads[2 * i + 1].wait()
+        for group in parts[part]:
+            average(groups.index(group))
+
     def ring_copy(owner, step, p, way):
-        i, first, size, _ = pieces[p]
-        which, c = groups[i]
+        which, c, n, first, size, _ = pieces[p]
         spot = pl.ds(pl.multiple_of(owner * rows + way * half + first, 16), size)
-        piece = ready[which].at[spot, columns(c)]
+        piece = ready[which].at[spot, columns(c, n)]
         return pltpu.make_async_remote_copy(
             src_ref=piece, dst_ref=piece,
-            send_sem=send_sem.at[way, lax.rem(step, 2), p], recv_sem=recv_sem.at[way, step, p],
+            send_sem=send_sem.at[way, lax.rem(step, 2), p],
+            recv_sem=recv_sem.at[way, lax.rem(step, 3), p],
+            device_id=(behind if way else ahead, side), device_id_type=MESH,
+        )
+
+    def raw_copy(way):
+        return pltpu.make_async_remote_copy(
+            src_ref=lk.at[pl.ds(way * half, raw_rows)], dst_ref=raw.at[way],
+            send_sem=raw_send.at[way], recv_sem=raw_recv.at[way],
             device_id=(behind if way else ahead, side), device_id_type=MESH,
         )
 
     def owner_of(step, way):
         return node(step if way else -step)
 
-    def send_own(i):
-        which, c = groups[i]
-        scale = scales[which][:, columns(c)]
-        for way in range(2):
-
-            def step(t, carry):
-                at = pl.multiple_of(way * half + t * tile, 16)
-                home = pl.multiple_of(me * rows + at, 16)
-                ready[which][pl.ds(home, tile), columns(c)] = (
-                    latest[which][pl.ds(at, tile), columns(c)] / scale
-                ).astype(jnp.bfloat16)
-                return carry
-
-            lax.fori_loop(0, half // tile, step, 0)
-            for p in range(len(pieces)):
-                if pieces[p][0] == i:
+    def send_own(part):
+        for p, (which, c, n, first, size, _) in enumerate(pieces):
+            if (which, c) not in parts[part]:
+                continue
+            for way in range(2):
+                for each in range(c, c + n):
+                    scale = scales[which][:, columns(each)]
+                    short = tile if size % tile == 0 else 16
+
+                    def step(t, carry):
+                        at = pl.multiple_of(way * half + first + t * short, 16)
+                        home = pl.multiple_of(me * rows + at, 16)
+                        ready[which][pl.ds(home, short), columns(each)] = (
+                            latest[which][pl.ds(at, short), columns(each)] / scale
+                        ).astype(jnp.bfloat16)
+                        return carry
+
+                    lax.fori_loop(0, size // short, step, 0)
+                if p:
                     allowed(p, lambda: ring_copy(me, 0, p, way).start())
 
     def tell(part):
@@ -179,36 +214,36 @@
             stat_copy(part, k).start()
 
     def finish(part):
-        first, last = parts[part]
-        for k in range(1, count):
-            stat_copy(part, k).wait_recv()
-        for i in range(first, last):
-            which, c = groups[i]
+        all_stats(part).wait_recv()
+        for group in parts[part]:
+            i = groups.index(group)
+            which, c = group
             total = stats[0, :, columns(i)]
             for k in range(1, count):
                 total = total + stats[k, :, columns(i)]
             scales[which][:, columns(c)] = jnp.sqrt(total)
 
-    for part, (first, last) in enumerate(parts):
-        for i in range(first, last):
-            average(i)
+    for part in range(len(parts)):
+        averages(part)
         if part == 0:
             pl.semaphore_wait(barrier, count + across - 2)
         tell(part)
         if part == 0:
+            for way in range(2):
+                raw_copy(way).start()
+            for load in norms:
+                load.wait()
+            norm_all[mine] = in_train[...] + in_step[...]
             for k in range(1, across):
-                near_copy(k).start()
+                near_copy(mine, k).start()
         else:
             finish(part - 1)
-            for i in range(*parts[part - 1]):
-                send_own(i)
+            send_own(part - 1)
     finish(len(parts) - 1)
-    for i in range(*parts[-1]):
-        send_own(i)
-    for k in range(1, across):
-        near_copy(k).wait_recv()
+    send_own(len(parts) - 1)
+    all_near.wait_recv()
     for k in range(1, count):
-        far_copy(k).start()
+        far_copy(pl.ds(me * across, across), k).start()
 
     def leave(step):
         for p in range(len(pieces)):
@@ -217,7 +252,26 @@
                 for way in range(2):
                     ring_copy(owner_of(step, way), step, p, way).wait_send()
 
-            allowed(p, left)
+            if p:
+                allowed(p, left)
+            else:
+                pl.when(step > 0)(left)
+
+    def pass_raw():
+        short = tile if raw_rows % tile == 0 else 16
+        for way in range(2):
+            raw_copy(way).wait_recv()
+            home = owner_of(1, way) * rows + way * half
+
+            def step(t, carry):
+                at = pl.ds(pl.multiple_of(t * short, 16), short)
+                rk[pl.ds(pl.multiple_of(home + t * short, 16), short), :] = (
+                    raw[way, at, :] / scale_k[...]
+                ).astype(jnp.bfloat16)
+                return carry
+
+            lax.fori_loop(0, raw_rows // short, step, 0)
+            ring_copy(owner_of(1, way), 1, 0, way).start()
 
     def forward(step, carry):
         owners = owner_of(step, 0), owner_of(step, 1)
@@ -228,17 +282,21 @@
                     ring_copy(owners[way], step - 1, p, way).wait_recv()
                     ring_copy(owners[way], step, p, way).start()
 
-            allowed(p, pass_on)
+            if p:
+                allowed(p, pass_on)
+            else:
+                pl.when(step > 1)(pass_on)
         leave(step - 1)
         return carry
 
+    pass_raw()
     lax.fori_loop(1, count - 1, forward, 0)
-    for k in range(1, count):
-        for part in range(len(parts)):
-            stat_copy(part, k).wait_send()
-        far_copy(k).wait()
-    for k in range(1, across):
-        near_copy(k).wait_send()
+    for way in range(2):
+        raw_copy(way).wait_send()
+    all_stats().wait_send()
+    all_near.wait_send()
+    all_far.wait_send()
+    all_far.wait_recv()
     for p in range(len(pieces)):
 
         def arrive():
@@ -257,21 +315,29 @@
     rows = arrays[0].shape[0]
     wides = [a.shape[1] for a in arrays[::2]]
     half = rows // 2
+    cut = cut_of(half)
+    raw_rows = min(cut, 160)
     width = wides[1]
     tile = 112 if half % 112 == 0 else 16
-    groups = [(1, 0)] + [(0, c) for c in range(wides[0] // width)] + [(2, 0)]
-    n = len(groups)
-    cut = cut_of(half)
-    pieces = [(i, 0, half, False) for i in range(1, n - 1)]
-    pieces = [(0, 0, cut, False), (0, cut, half - cut, True)] + pieces + [(n - 1, 0, half, True)]
-    parts = [(0, 2), (2, 5), (5, n)]
+    n = wides[0] // width
+    a, b = 1, (n + 1) // 2
+    spans = [(0, 0, a), (0, a, b - a), (0, b, n - b)]
+    parts = [[(which, c + i) for i in range(m)] for which, c, m in spans]
+    parts[0].append((1, 0))
+    parts[2].append((2, 0))
+    batches = [(0, 1, 0, 1)] + [(i, *span) for i, span in enumerate(spans)] + [(2, 2, 0, 1)]
+    pieces = [(1, 0, 1, 0, raw_rows, False), (*spans[0], 0, half, False)]
+    pieces += [(1, 0, 1, raw_rows, cut - raw_rows, False), (1, 0, 1, cut, half - cut, True)]
+    pieces += [(*span, 0, half, False) for span in spans[1:]] + [(2, 0, 1, 0, half, True)]
     piece = norm_train.shape[0]
     hbm = pl.BlockSpec(memory_space=pl.ANY)
     vmem = pl.BlockSpec(memory_space=pltpu.VMEM)
     dma = pltpu.SemaphoreType.DMA
     return pl.pallas_call(
-        functools.partial(gather_kernel, count, across, width, half, tile, groups, parts, pieces),
-        in_specs=[hbm] * 6 + [vmem] * 2,
+        functools.partial(
+            gather_kernel, count, across, width, half, tile, raw_rows, parts, batches, pieces
+        ),
+        in_specs=[hbm] * 8,
         out_specs=[vmem] * 10,
         out_shape=[pltpu.VMEM((count * rows, w), jnp.bfloat16) for w in wides]
         + [pltpu.VMEM((rows, w), jnp.float32) for w in wides]
@@ -279,16 +345,20 @@
         + [pltpu.VMEM((count * across, 1, piece), jnp.float32)],
         scratch_shapes=[pltpu.VMEM(a.shape, jnp.float32) for a in arrays]
         + [
-            pltpu.VMEM((count, 1, n * width), jnp.float32),
-            dma((2, n)),
-            dma((len(parts), count - 1)),
-            dma((len(parts), count - 1)),
-            dma((across - 1,)),
-            dma((across - 1,)),
-            dma((count - 1,)),
-            dma((count - 1,)),
+            pltpu.VMEM((1, piece), jnp.float32),
+            pltpu.VMEM((1, piece), jnp.float32),
+            pltpu.VMEM((count, 1, sum(wides)), jnp.float32),
+            pltpu.VMEM((2, raw_rows, width), jnp.float32),
+            dma((len(batches), 2)),
+            dma((2,)),
+            dma((1,)),
+            dma((len(parts),)),
+            dma((2,)),
+            dma((2,)),
+            dma((2,)),
+            dma((2,)),
             dma((2, 2, len(pieces))),
-            dma((2, count - 1, len(pieces))),
+            dma((2, 3, len(pieces))),
         ],
         compiler_params=pltpu.CompilerParams(
             collective_id=0, has_side_effects=True,
@@ -324,7 +394,7 @@
     out_rk, out_rv, out_lq, out_lk, out_lv, out_sq, out_sk, out_sv, out_norm,
     sem, key_sem, own_sem,
 ):
-    late = lax.rem(lax.axis_index("width"), 2) == 0
+    late = lax.rem(lax.axis_index("width"), 2) == 1
     rows = rv.shape[0] // count
     base = lax.axis_index("zero") * rows
     half = rows // 2
@@ -422,7 +492,7 @@
         piece = ref.at[pl.ds(pl.multiple_of((owner * 2 + way) * size + first, 16), tile)]
         return pltpu.make_async_remote_copy(
             src_ref=piece, dst_ref=piece,
-            send_sem=send_sem.at[way, lax.rem(step, 2), p], recv_sem=recv_sem.at[way, step, p],
+            send_sem=send_sem.at[way, lax.rem(step, 2), p], recv_sem=recv_sem.at[way, lax.rem(step, 3), p],
             device_id=(behind if way else ahead, side), device_id_type=MESH,
         )
 
@@ -434,7 +504,7 @@
             for way in range(2):
                 ring_copy(owner_of(step, way), step, p, way).wait_send()
 
-    @pl.when(lax.rem(side, 2) == 0)
+    @pl.when(lax.rem(side, 2) == 1)
     def _():
         barrier = pltpu.get_barrier_semaphore()
         for other in (ahead, behind):
@@ -486,7 +556,7 @@
             pltpu.VMEM((2 * count * rest, own_k.shape[1]), own_k.dtype),
             pltpu.VMEM(own_v.shape, own_v.dtype),
         ],
-        scratch_shapes=[dma((2, 2)), dma((2, 2, n)), dma((2, count - 1, n))],
+        scratch_shapes=[dma((2, 2)), dma((2, 2, n)), dma((2, 3, n))],
         compiler_params=pltpu.CompilerParams(
             collective_id=1, has_side_effects=True, vmem_limit_bytes=56 * 2**20
         ),
@@ -494,19 +564,20 @@
 
 
 def store_late_kernel(count, cuts, rk, rv, start_k, start_v, out_k, out_v, sem, key_sem):
-    @pl.when(lax.rem(lax.axis_index("width"), 2) == 0)
+    @pl.when(lax.rem(lax.axis_index("width"), 2) == 1)
     def _():
         copies = pieces_of(rv, out_v, sem, cuts)
-        for i, (here, there) in enumerate(key_pieces(count, rv.shape[0] // count, True, True)):
-            copies.append(pltpu.make_async_copy(rk.at[here], out_k.at[there], key_sem.at[i]))
         for copy in copies:
             copy.start()
+        for here, there in key_pieces(count, rv.shape[0] // count, True, True):
+            pltpu.make_async_copy(rk.at[here], out_k.at[there], key_sem).start()
         for copy in copies:
             copy.wait()
+        pltpu.make_async_copy(rk, out_k.at[pl.ds(0, rk.shape[0])], key_sem).wait()
 
 
 def store_late(rk, rv, start_k, start_v, count):
-    cuts = 8
+    cuts = 4
     hbm = pl.BlockSpec(memory_space=pltpu.HBM)
     vmem = pl.BlockSpec(memory_space=pltpu.VMEM)
     dma = pltpu.SemaphoreType.DMA
@@ -515,7 +586,7 @@
         in_specs=[vmem] * 2 + [hbm] * 2,
         out_specs=[hbm] * 2,
         out_shape=[jax.ShapeDtypeStruct(a.shape, a.dtype) for a in (start_k, start_v)],
-        scratch_shapes=[dma((cuts,)), dma((2 * count,))],
+        scratch_shapes=[dma((cuts,)), dma],
         input_output_aliases={2: 0, 3: 1},
         compiler_params=pltpu.CompilerParams(vmem_limit_bytes=40 * 2**20),
     )(rk, rv, start_k, start_v)

time: 326 us -> 323 us (level)
  Pallas kernels: 325 us -> 319 us
    pallas_call x1, Pallas kernels: 34 us -> 0.57 us  [gather_late(): pl.pallas_call(functools.partial(late_kernel, count, half, tile), in_spec...]
    pallas_call x1, Pallas kernels: 274 us -> 303 us  [gather(): pl.pallas_call(functools.partial(gather_kernel, count, across, width, hal...]
where the time goes in v3:
time: 323 us; the launch traced here: 321 us
  Pallas kernels  319 us (99%)
    pallas_call x1, Pallas kernels, gather(): pl.pallas_call(functools.partial(gather_kernel, count, across, width, hal...  303 us
    pallas_call x1, Pallas kernels, store_one(): pl.pallas_call(functools.partial(store_one_kernel, cuts), in_specs=[pl.Bl...  8.7 us
    pallas_call x1, Pallas kernels, store(): pl.pallas_call(functools.partial(store_kernel, count, cuts), in_specs=[vm...  6.59 us

profile of v3, /device:TPU:0, one launch (start us, length us, event | category | flops | bytes accessed | tf_op | source)
XLA Modules:
  0.0 320.7 jit_solution(15484771695785378327)
XLA Ops:
  0.6 303.3 %shard_map.159 = (bf16[7168,1792]{1,0:T(8,128)(2,1)S(1)}, bf16[7168,256]{1,0:T(8,128)(2,1)S(1)}, bf16[7168,256]{1,0:T(8,128)(2,1)S(1)}, f32[896,1792]{1,0:T(8,12...) custom-call(f32[896,1792]{1,0:T(8,128)} %tq.1, ...), custom_call_target="tpu_custom_call" | custom-call | tf_op jit(solution)/shard_map/pallas_call | solution.py:336
  303.9 8.7 %shard_map.160.rq = bf16[7168,1792]{1,0:T(8,128)(2,1)} custom-call(bf16[7168,1792]{1,0:T(8,128)(2,1)S(1)} %get-tuple-element.33.source), custom_call_target="tpu_custom_call" | custom-call | tf_op jit(solution)/shard_map/pallas_call | solution.py:471
  312.6 6.6 %shard_map.161 = (bf16[7168,256]{1,0:T(8,128)(2,1)}, bf16[7168,256]{1,0:T(8,128)(2,1)}, f32[896,1792]{1,0:T(8,128)}, f32[896,256]{1,0:T(8,128)}, f32[896,256]{1,...) custom-call(bf16[7168,256]{1,0:T(8,128)(2,1)S(1)} %get-tuple-element.34.rk, ...), custom_call_target="tpu_custom_call" | custom-call | tf_op jit(solution)/shard_map/pallas_call | solution.py:449
  319.2 0.1 reduce
  319.3 0.7 reshape.31.after
  320.0 0.6 shard_map.162
  320.6 0.1 shard_map.163

commit v4 on v3

--- a/solution.py
+++ b/solution.py
@@ -173,7 +173,7 @@
         piece = ready[which].at[spot, columns(c, n)]
         return pltpu.make_async_remote_copy(
             src_ref=piece, dst_ref=piece,
-            send_sem=send_sem.at[way, lax.rem(step, 2), p],
+            send_sem=send_sem.at[way, lax.rem(step, 2)],
             recv_sem=recv_sem.at[way, lax.rem(step, 3), p],
             device_id=(behind if way else ahead, side), device_id_type=MESH,
         )
@@ -246,16 +246,18 @@
         far_copy(pl.ds(me * across, across), k).start()
 
     def leave(step):
-        for p in range(len(pieces)):
-
-            def left():
-                for way in range(2):
-                    ring_copy(owner_of(step, way), step, p, way).wait_send()
-
-            if p:
-                allowed(p, left)
-            else:
-                pl.when(step > 0)(left)
+        def left(n):
+            whole = rk.at[pl.ds(0, n)]
+            for way in range(2):
+                pltpu.make_async_remote_copy(
+                    src_ref=whole, dst_ref=whole, send_sem=send_sem.at[way, lax.rem(step, 2)],
+                    recv_sem=recv_sem.at[way, 0, 0], device_id=(ahead, side), device_id_type=MESH,
+                ).wait_send()
+
+        for kind in (late, jnp.logical_not(late)):
+            n = sum(p[2] * p[4] for p in pieces if kind is not late or not p[5])
+            pl.when(jnp.logical_and(kind, step > 0))(functools.partial(left, n))
+            pl.when(jnp.logical_and(kind, step == 0))(functools.partial(left, n - raw_rows))
 
     def pass_raw():
         short = tile if raw_rows % tile == 0 else 16
@@ -308,7 +310,7 @@
 
 
 def cut_of(half):
-    return half // 32 * 16
+    return half // 4 * 3
 
 
 def gather(arrays, norm_train, norm_step, count, across):
@@ -357,7 +359,7 @@
             dma((2,)),
             dma((2,)),
             dma((2,)),
-            dma((2, 2, len(pieces))),
+            dma((2, 2)),
             dma((2, 3, len(pieces))),
         ],
         compiler_params=pltpu.CompilerParams(
@@ -376,16 +378,9 @@
     return copies
 
 
-def key_pieces(count, rows, late, small):
+def early_key(count, rows):
     half = rows // 2
-    cut = cut_of(half)
-    size = half - cut if late else cut
-    pieces = []
-    for owner in range(count):
-        for way in range(2):
-            spot = pl.ds(owner * rows + way * half + (cut if late else 0), size)
-            pieces.append((pl.ds((owner * 2 + way) * size, size) if small else spot, spot))
-    return pieces
+    return [pl.ds(i * half, cut_of(half)) for i in range(2 * count)]
 
 
 def store_kernel(
@@ -403,7 +398,7 @@
     for i, (source, target) in enumerate(((lq, out_lq), (lk, out_lk), (lv, out_lv))):
         both += pieces_of(source, target, sem.at[i], cuts)
     first += pieces_of(rk, out_rk, sem.at[3], cuts) + pieces_of(rv, out_rv, sem.at[4], cuts)
-    for i, (_, at) in enumerate(key_pieces(count, rows, False, False)):
+    for i, at in enumerate(early_key(count, rows)):
         last.append(pltpu.make_async_copy(rk.at[at], out_rk.at[at], key_sem.at[i]))
     at = pl.ds(pl.multiple_of(base, 16), rows)
     last.append(pltpu.make_async_copy(rv.at[at], out_rv.at[at], own_sem.at[0]))
@@ -492,7 +487,7 @@
         piece = ref.at[pl.ds(pl.multiple_of((owner * 2 + way) * size + first, 16), tile)]
         return pltpu.make_async_remote_copy(
             src_ref=piece, dst_ref=piece,
-            send_sem=send_sem.at[way, lax.rem(step, 2), p], recv_sem=recv_sem.at[way, lax.rem(step, 3), p],
+            send_sem=send_sem.at[way, lax.rem(step, 2)], recv_sem=recv_sem.at[way, lax.rem(step, 3), p],
             device_id=(behind if way else ahead, side), device_id_type=MESH,
         )
 
@@ -500,9 +495,12 @@
         return node(step if way else -step)
 
     def leave(step):
-        for p in range(len(pieces)):
-            for way in range(2):
-                ring_copy(owner_of(step, way), step, p, way).wait_send()
+        whole = rv.at[pl.ds(0, rest + half)]
+        for way in range(2):
+            pltpu.make_async_remote_copy(
+                src_ref=whole, dst_ref=whole, send_sem=send_sem.at[way, lax.rem(step, 2)],
+                recv_sem=recv_sem.at[way, 0, 0], device_id=(ahead, side), device_id_type=MESH,
+            ).wait_send()
 
     @pl.when(lax.rem(side, 2) == 1)
     def _():
@@ -556,37 +554,43 @@
             pltpu.VMEM((2 * count * rest, own_k.shape[1]), own_k.dtype),
             pltpu.VMEM(own_v.shape, own_v.dtype),
         ],
-        scratch_shapes=[dma((2, 2)), dma((2, 2, n)), dma((2, 3, n))],
+        scratch_shapes=[dma((2, 2)), dma((2, 2)), dma((2, 3, n))],
         compiler_params=pltpu.CompilerParams(
             collective_id=1, has_side_effects=True, vmem_limit_bytes=56 * 2**20
         ),
     )(own_k, own_v, after)
 
 
-def store_late_kernel(count, cuts, rk, rv, start_k, start_v, out_k, out_v, sem, key_sem):
-    @pl.when(lax.rem(lax.axis_index("width"), 2) == 1)
+def store_late_kernel(count, rk, rv, start_k, start_v, out_k, out_v, sem):
+    me, side = lax.axis_index("zero"), lax.axis_index("width")
+    rows, rest = rv.shape[0] // count, rk.shape[0] // count // 2
+    half = rows // 2
+
+    @pl.when(lax.rem(side, 2) == 1)
     def _():
-        copies = pieces_of(rv, out_v, sem, cuts)
-        for copy in copies:
-            copy.start()
-        for here, there in key_pieces(count, rv.shape[0] // count, True, True):
-            pltpu.make_async_copy(rk.at[here], out_k.at[there], key_sem).start()
-        for copy in copies:
-            copy.wait()
-        pltpu.make_async_copy(rk, out_k.at[pl.ds(0, rk.shape[0])], key_sem).wait()
+        for k in range(1, count):
+            owner = lax.rem(me + k, count)
+            at = pl.ds(pl.multiple_of(owner * rows, 16), rows)
+            pltpu.make_async_copy(rv.at[at], out_v.at[at], sem.at[0]).start()
+            for way in range(2):
+                here = pl.ds(pl.multiple_of((owner * 2 + way) * rest, 16), rest)
+                there = pl.ds(pl.multiple_of(owner * rows + way * half + half - rest, 16), rest)
+                pltpu.make_async_copy(rk.at[here], out_k.at[there], sem.at[1]).start()
+        for i, (near, far) in enumerate(((rv, out_v), (rk, out_k))):
+            n = near.shape[0] // count * (count - 1)
+            pltpu.make_async_copy(near.at[pl.ds(0, n)], far.at[pl.ds(0, n)], sem.at[i]).wait()
 
 
 def store_late(rk, rv, start_k, start_v, count):
-    cuts = 4
     hbm = pl.BlockSpec(memory_space=pltpu.HBM)
     vmem = pl.BlockSpec(memory_space=pltpu.VMEM)
     dma = pltpu.SemaphoreType.DMA
     return pl.pallas_call(
-        functools.partial(store_late_kernel, count, cuts),
+        functools.partial(store_late_kernel, count),
         in_specs=[vmem] * 2 + [hbm] * 2,
         out_specs=[hbm] * 2,
         out_shape=[jax.ShapeDtypeStruct(a.shape, a.dtype) for a in (start_k, start_v)],
-        scratch_shapes=[dma((cuts,)), dma],
+        scratch_shapes=[dma((2,))],
         input_output_aliases={2: 0, 3: 1},
         compiler_params=pltpu.CompilerParams(vmem_limit_bytes=40 * 2**20),
     )(rk, rv, start_k, start_v)

time: 323 us -> 323 us (level)
  no operation moved by 1% of the time
where the time goes in v4:
time: 323 us; the launch traced here: 320 us
  Pallas kernels  319 us (99%)
    pallas_call x1, Pallas kernels, gather(): pl.pallas_call(functools.partial(gather_kernel, count, across, width, hal...  303 us
    pallas_call x1, Pallas kernels, store_one(): pl.pallas_call(functools.partial(store_one_kernel, cuts), in_specs=[pl.Bl...  8.7 us
    pallas_call x1, Pallas kernels, store(): pl.pallas_call(functools.partial(store_kernel, count, cuts), in_specs=[vm...  6.59 us

profile of v4, /device:TPU:0, one launch (start us, length us, event | category | flops | bytes accessed | tf_op | source)
XLA Modules:
  0.0 320.2 jit_solution(5489110232637440895)
XLA Ops:
  0.6 303.1 %shard_map.159 = (bf16[7168,1792]{1,0:T(8,128)(2,1)S(1)}, bf16[7168,256]{1,0:T(8,128)(2,1)S(1)}, bf16[7168,256]{1,0:T(8,128)(2,1)S(1)}, f32[896,1792]{1,0:T(8,12...) custom-call(f32[896,1792]{1,0:T(8,128)} %tq.1, ...), custom_call_target="tpu_custom_call" | custom-call | tf_op jit(solution)/shard_map/pallas_call | solution.py:338
  303.7 8.7 %shard_map.160.rq = bf16[7168,1792]{1,0:T(8,128)(2,1)} custom-call(bf16[7168,1792]{1,0:T(8,128)(2,1)S(1)} %get-tuple-element.33.source), custom_call_target="tpu_custom_call" | custom-call | tf_op jit(solution)/shard_map/pallas_call | solution.py:466
  312.4 6.6 %shard_map.161 = (bf16[7168,256]{1,0:T(8,128)(2,1)}, bf16[7168,256]{1,0:T(8,128)(2,1)}, f32[896,1792]{1,0:T(8,128)}, f32[896,256]{1,0:T(8,128)}, f32[896,256]{1,...) custom-call(bf16[7168,256]{1,0:T(8,128)(2,1)S(1)} %get-tuple-element.34.rk, ...), custom_call_target="tpu_custom_call" | custom-call | tf_op jit(solution)/shard_map/pallas_call | solution.py:444
  319.0 0.1 reduce
  319.1 0.7 reshape.31.after
  319.8 0.3 shard_map.162
  (1 shorter events, 0.0 us)

commit v5 on v4

--- a/solution.py
+++ b/solution.py
@@ -310,7 +310,7 @@
 
 
 def cut_of(half):
-    return half // 4 * 3
+    return half - (112 if half % 112 == 0 and half > 112 else half // 64 * 16)
 
 
 def gather(arrays, norm_train, norm_step, count, across):
@@ -318,7 +318,7 @@
     wides = [a.shape[1] for a in arrays[::2]]
     half = rows // 2
     cut = cut_of(half)
-    raw_rows = min(cut, 160)
+    raw_rows = cut // 32 * 16
     width = wides[1]
     tile = 112 if half % 112 == 0 else 16
     n = wides[0] // width

time: 323 us -> 323 us (level)
  no operation moved by 1% of the time
where the time goes in v5:
time: 323 us; the launch traced here: 320 us
  Pallas kernels  319 us (99%)
    pallas_call x1, Pallas kernels, gather(): pl.pallas_call(functools.partial(gather_kernel, count, across, width, hal...  303 us
    pallas_call x1, Pallas kernels, store_one(): pl.pallas_call(functools.partial(store_one_kernel, cuts), in_specs=[pl.Bl...  8.7 us
    pallas_call x1, Pallas kernels, store(): pl.pallas_call(functools.partial(store_kernel, count, cuts), in_specs=[vm...  6.59 us

profile of v5, /device:TPU:0, one launch (start us, length us, event | category | flops | bytes accessed | tf_op | source)
XLA Modules:
  0.0 320.2 jit_solution(5489110232637440895)
XLA Ops:
  0.6 303.1 %shard_map.159 = (bf16[7168,1792]{1,0:T(8,128)(2,1)S(1)}, bf16[7168,256]{1,0:T(8,128)(2,1)S(1)}, bf16[7168,256]{1,0:T(8,128)(2,1)S(1)}, f32[896,1792]{1,0:T(8,12...) custom-call(f32[896,1792]{1,0:T(8,128)} %tq.1, ...), custom_call_target="tpu_custom_call" | custom-call | tf_op jit(solution)/shard_map/pallas_call | solution.py:338
  303.7 8.7 %shard_map.160.rq = bf16[7168,1792]{1,0:T(8,128)(2,1)} custom-call(bf16[7168,1792]{1,0:T(8,128)(2,1)S(1)} %get-tuple-element.33.source), custom_call_target="tpu_custom_call" | custom-call | tf_op jit(solution)/shard_map/pallas_call | solution.py:466
  312.4 6.6 %shard_map.161 = (bf16[7168,256]{1,0:T(8,128)(2,1)}, bf16[7168,256]{1,0:T(8,128)(2,1)}, f32[896,1792]{1,0:T(8,128)}, f32[896,256]{1,0:T(8,128)}, f32[896,256]{1,...) custom-call(bf16[7168,256]{1,0:T(8,128)(2,1)S(1)} %get-tuple-element.34.rk, ...), custom_call_target="tpu_custom_call" | custom-call | tf_op jit(solution)/shard_map/pallas_call | solution.py:444
  319.0 0.1 reduce
  319.1 0.7 reshape.31.after
  319.8 0.3 shard_map.162
  (1 shorter events, 0.0 us)

commit v6 on v5

--- a/solution.py
+++ b/solution.py
@@ -189,7 +189,8 @@
         return node(step if way else -step)
 
     def send_own(part):
-        for p, (which, c, n, first, size, _) in enumerate(pieces):
+        for p in (*range(1, len(pieces)), 0):
+            which, c, n, first, size, _ = pieces[p]
             if (which, c) not in parts[part]:
                 continue
             for way in range(2):

time: 323 us -> 323 us (level)
  no operation moved by 1% of the time
where the time goes in v6:
time: 323 us; the launch traced here: 320 us
  Pallas kernels  319 us (99%)
    pallas_call x1, Pallas kernels, gather(): pl.pallas_call(functools.partial(gather_kernel, count, across, width, hal...  303 us
    pallas_call x1, Pallas kernels, store_one(): pl.pallas_call(functools.partial(store_one_kernel, cuts), in_specs=[pl.Bl...  8.7 us
    pallas_call x1, Pallas kernels, store(): pl.pallas_call(functools.partial(store_kernel, count, cuts), in_specs=[vm...  6.59 us

profile of v6, /device:TPU:0, one launch (start us, length us, event | category | flops | bytes accessed | tf_op | source)
XLA Modules:
  0.0 320.0 jit_solution(9582324455758779320)
XLA Ops:
  0.6 302.9 %shard_map.159 = (bf16[7168,1792]{1,0:T(8,128)(2,1)S(1)}, bf16[7168,256]{1,0:T(8,128)(2,1)S(1)}, bf16[7168,256]{1,0:T(8,128)(2,1)S(1)}, f32[896,1792]{1,0:T(8,12...) custom-call(f32[896,1792]{1,0:T(8,128)} %tq.1, ...), custom_call_target="tpu_custom_call" | custom-call | tf_op jit(solution)/shard_map/pallas_call | solution.py:339
  303.5 8.7 %shard_map.160.rq = bf16[7168,1792]{1,0:T(8,128)(2,1)} custom-call(bf16[7168,1792]{1,0:T(8,128)(2,1)S(1)} %get-tuple-element.33.source), custom_call_target="tpu_custom_call" | custom-call | tf_op jit(solution)/shard_map/pallas_call | solution.py:467
  312.2 6.6 %shard_map.161 = (bf16[7168,256]{1,0:T(8,128)(2,1)}, bf16[7168,256]{1,0:T(8,128)(2,1)}, f32[896,1792]{1,0:T(8,128)}, f32[896,256]{1,0:T(8,128)}, f32[896,256]{1,...) custom-call(bf16[7168,256]{1,0:T(8,128)(2,1)S(1)} %get-tuple-element.34.rk, ...), custom_call_target="tpu_custom_call" | custom-call | tf_op jit(solution)/shard_map/pallas_call | solution.py:445
  318.8 0.1 reduce
  318.9 0.7 reshape.31.after
  319.6 0.3 shard_map.162
  (1 shorter events, 0.0 us)

commit v7 on v6

--- a/solution.py
+++ b/solution.py
@@ -311,7 +311,7 @@
 
 
 def cut_of(half):
-    return half - (112 if half % 112 == 0 and half > 112 else half // 64 * 16)
+    return half // 7 * 6 if half % 112 == 0 else half - half // 64 * 16
 
 
 def gather(arrays, norm_train, norm_step, count, across):
@@ -319,7 +319,7 @@
     wides = [a.shape[1] for a in arrays[::2]]
     half = rows // 2
     cut = cut_of(half)
-    raw_rows = cut // 32 * 16
+    raw_rows = min(160, cut // 32 * 16)
     width = wides[1]
     tile = 112 if half % 112 == 0 else 16
     n = wides[0] // width
@@ -542,7 +542,7 @@
 def gather_late(own_k, own_v, after, count):
     half = own_k.shape[0] // count // 2
     rest = half - cut_of(half)
-    tile = 112 if rest % 112 == 0 and half % 112 == 0 else 16
+    tile = rest if half % 112 == 0 else 16
     n = (rest + half) // tile
     hbm = pl.BlockSpec(memory_space=pltpu.HBM)
     vmem = pl.BlockSpec(memory_space=pltpu.VMEM)

time: 323 us -> 323 us (level)
  no operation moved by 1% of the time
where the time goes in v7:
time: 323 us; the launch traced here: 320 us
  Pallas kernels  319 us (99%)
    pallas_call x1, Pallas kernels, gather(): pl.pallas_call(functools.partial(gather_kernel, count, across, width, hal...  303 us
    pallas_call x1, Pallas kernels, store_one(): pl.pallas_call(functools.partial(store_one_kernel, cuts), in_specs=[pl.Bl...  8.7 us
    pallas_call x1, Pallas kernels, store(): pl.pallas_call(functools.partial(store_kernel, count, cuts), in_specs=[vm...  6.59 us

profile of v7, /device:TPU:0, one launch (start us, length us, event | category | flops | bytes accessed | tf_op | source)
XLA Modules:
  0.0 320.1 jit_solution(12611876972099503124)
XLA Ops:
  0.6 302.8 %shard_map.159 = (bf16[7168,1792]{1,0:T(8,128)(2,1)S(1)}, bf16[7168,256]{1,0:T(8,128)(2,1)S(1)}, bf16[7168,256]{1,0:T(8,128)(2,1)S(1)}, f32[896,1792]{1,0:T(8,12...) custom-call(f32[896,1792]{1,0:T(8,128)} %tq.1, ...), custom_call_target="tpu_custom_call" | custom-call | tf_op jit(solution)/shard_map/pallas_call | solution.py:339
  303.4 8.7 %shard_map.160.rq = bf16[7168,1792]{1,0:T(8,128)(2,1)} custom-call(bf16[7168,1792]{1,0:T(8,128)(2,1)S(1)} %get-tuple-element.33.source), custom_call_target="tpu_custom_call" | custom-call | tf_op jit(solution)/shard_map/pallas_call | solution.py:467
  312.2 6.6 %shard_map.161 = (bf16[7168,256]{1,0:T(8,128)(2,1)}, bf16[7168,256]{1,0:T(8,128)(2,1)}, f32[896,1792]{1,0:T(8,128)}, f32[896,256]{1,0:T(8,128)}, f32[896,256]{1,...) custom-call(bf16[7168,256]{1,0:T(8,128)(2,1)S(1)} %get-tuple-element.34.rk, ...), custom_call_target="tpu_custom_call" | custom-call | tf_op jit(solution)/shard_map/pallas_call | solution.py:445
  318.7 0.1 reduce
  318.8 0.7 reshape.31.after
  319.5 0.5 shard_map.162
  (1 shorter events, 0.0 us)
